TPU v7x, 128 devices: a whole 4x4x4 slice. The times are simulated.
128 devices in a mesh: ep: 8 (over z, core), fsdp: 16 (over y, x).
Axes of the slice: x: 4, y: 4, z: 4, core: 2. Of those that a mesh axis runs over, the one named last changes fastest.
Arguments:
- train_gate: float32 [64, 2048, 1408], P('ep', 'fsdp'), may hold values from -0.1875 to 0.1875
- train_up: float32 [64, 2048, 1408], P('ep', 'fsdp'), may hold values from -0.1875 to 0.1875
- train_down: float32 [64, 1408, 2048], P('ep', None, 'fsdp'), may hold values from -0.21875 to 0.21875
- router_weight: float32 [2048, 64], P('fsdp', 'ep'), may hold values from -0.125 to 0.125
- router_gain: float32 [2048], P('fsdp'), may hold values from 0.25 to 1.75
Outputs:
- ready_gate: bfloat16 [64, 2048, 1408], P('ep', None, 'fsdp')
- ready_up: bfloat16 [64, 2048, 1408], P('ep', None, 'fsdp')
- ready_down: bfloat16 [64, 1408, 2048], P('ep', 'fsdp')
- scale_gate: float32 [64, 1408], P('ep', 'fsdp')
- scale_up: float32 [64, 1408], P('ep', 'fsdp')
- scale_down: float32 [64, 1408], P('ep', 'fsdp')
- serve_router: bfloat16 [2048, 64], replicated
All inputs are finite; a program needn't handle non-finite values. Where the computation divides by a largest or mean magnitude, that divisor is 1e-20 or more.
Results may differ from a plain program's by a relative error of at most 0.012.
Values may be sent and summed in bfloat16 or wider, within the bound.
No kernel may reach another device: no remote copies, remote signals or barrier semaphores. Data moves between devices by JAX's collectives and lax.ppermute only.
A program may use at most 128 MiB of HBM per device.

v0:
```python
import jax
import jax.numpy as jnp
from jax import lax
from jax.sharding import PartitionSpec as P

D_MODEL = 2048


def sent_to_all(shard, axis):
    copies = jnp.broadcast_to(shard, (lax.axis_size(axis), *shard.shape))
    return lax.all_to_all(copies, axis, split_axis=0, concat_axis=0, tiled=True)


def over_copies(shard, axis):
    everything = sent_to_all(shard, axis)
    return jnp.sum(everything.astype(jnp.float32), axis=0)


def in_one_piece(arrays, axis, split_dim, concat_dim, along):
    ends, at = ([], 0)
    for a in arrays[:-1]:
        at += a.shape[along]
        ends.append(at)
    both = jnp.concatenate(arrays, axis=along)
    return tuple(
        jnp.split(
            lax.all_to_all(both, axis, split_axis=split_dim, concat_axis=concat_dim, tiled=True),
            ends,
            axis=along,
        )
    )


def split_up(shard, dim, size):
    before, after = (shard.shape[:dim], shard.shape[dim + 1 :])
    return jnp.moveaxis(shard.reshape(*before, size, -1, *after), dim, 0)


def edges_of(length, count):
    step = length // count
    if step >= 8:
        step -= step % 8
    return [step * k for k in range(1, count)]


def laid_out(parts, dim):
    shape = list(parts.shape[1:])
    shape[dim] *= parts.shape[0]
    return jnp.moveaxis(parts, 0, dim).reshape(shape)


def exchange_in_pieces(shard, axis, pieces, split_dim, concat_dim):
    parts = split_up(shard, split_dim, lax.axis_size(axis))
    split_at = max(range(1, max(2, parts.ndim - 1)), key=lambda d: parts.shape[d])
    finished = []
    for section in jnp.split(parts, edges_of(parts.shape[split_at], pieces), axis=split_at):
        if section.size:
            finished.append(lax.all_to_all(section, axis, split_axis=0, concat_axis=0, tiled=True))
    return laid_out(jnp.concatenate(finished, axis=split_at), concat_dim)


def collect(shard, axis, dim):
    return laid_out(sent_to_all(shard, axis), dim)


def shards(train_gate, train_up, train_down, router_weight, router_gain):
    total_gate, total_up, total_down = (
        over_copies(jnp.sum(jnp.abs(train_gate), axis=1).astype(jnp.bfloat16), "fsdp").astype(
            jnp.float32
        ),
        over_copies(jnp.sum(jnp.abs(train_up), axis=1).astype(jnp.bfloat16), "fsdp").astype(
            jnp.float32
        ),
        over_copies(jnp.sum(jnp.abs(train_down), axis=2).astype(jnp.bfloat16), "fsdp").astype(
            jnp.float32
        ),
    )
    scale_gate = total_gate / D_MODEL
    scale_up = total_up / D_MODEL
    scale_down = total_down / D_MODEL
    narrow_gate, narrow_up, narrow_down = (
        (train_gate / jnp.expand_dims(scale_gate, 1)).astype(jnp.bfloat16),
        (train_up / jnp.expand_dims(scale_up, 1)).astype(jnp.bfloat16),
        (train_down / jnp.expand_dims(scale_down, 2)).astype(jnp.bfloat16),
    )
    ready_gate, ready_up = in_one_piece((narrow_gate, narrow_up), "fsdp", 2, 1, 0)
    ready_down = exchange_in_pieces(narrow_down, "fsdp", 2, 1, 2)
    scale_gate = lax.dynamic_slice_in_dim(
        scale_gate, lax.axis_index("fsdp") * ready_gate.shape[2], ready_gate.shape[2], axis=1
    )
    scale_up = lax.dynamic_slice_in_dim(
        scale_up, lax.axis_index("fsdp") * ready_up.shape[2], ready_up.shape[2], axis=1
    )
    scale_down = lax.dynamic_slice_in_dim(
        scale_down, lax.axis_index("fsdp") * ready_down.shape[1], ready_down.shape[1], axis=1
    )
    part_router = (router_weight * router_gain[:, None]).astype(jnp.bfloat16)
    row_router = collect(part_router, "fsdp", 0)
    serve_router = collect(row_router, "ep", 1)
    return (ready_gate, ready_up, ready_down, scale_gate, scale_up, scale_down, serve_router)


def solution(mesh):
    in_specs = (
        P("ep", "fsdp", None),
        P("ep", "fsdp", None),
        P("ep", None, "fsdp"),
        P("fsdp", "ep"),
        P("fsdp"),
    )
    out_specs = (
        P("ep", None, "fsdp"),
        P("ep", None, "fsdp"),
        P("ep", "fsdp", None),
        P("ep", "fsdp"),
        P("ep", "fsdp"),
        P("ep", "fsdp"),
        P(),
    )
    return jax.shard_map(shards, mesh=mesh, in_specs=in_specs, out_specs=out_specs, check_vma=False)
```

profile of v0, /device:TPU:8, one launch (start us, length us, event | category | flops | bytes accessed | tf_op | source)
XLA Modules:
  0.0 217.4 jit_solution(6295316721826833313)
XLA Ops:
  0.6 0.7 multiply_convert_fusion
  1.3 0.6 broadcast_in_dim.22
  1.9 7.4 %all-to-all-start.6 = ((bf16[16,128,8]{1,2,0:T(8,128)(2,1)}), bf16[16,128,8]{1,2,0:T(8,128)(2,1)S(1)}, u32[]{:S(2)}, u32[]{:S(2)}) async-start(bf16[16,128,8]{1,2,0:T(8,128)(2,1)} %broadcast_in_dim.22), calls=%async_computation.6 | async-start | bytes 65536 | tf_op jit(solution)/shard_map/all_to_all | solution.py:11
  9.3 4.2 %abs_reduce_fusion = bf16[8,1408]{1,0:T(8,128)(2,1)S(1)} fusion(f32[8,1408,128]{2,1,0:T(8,128)} %param.7), kind=kLoop, calls=%fused_computation.2 | loop fusion | flops 2872320 | bytes 5789696 | tf_op jit(solution)/shard_map/reduce_sum | solution.py:74
  13.5 2.0 all-to-all-done.6
  15.6 0.8 broadcast_in_dim.21
  16.3 5.2 %all-to-all-start.3 = ((bf16[16,8,1408]{2,1,0:T(8,128)(2,1)}), bf16[16,8,1408]{2,1,0:T(8,128)(2,1)S(1)}, u32[]{:S(2)}, u32[]{:S(2)}) async-start(bf16[16,8,1408]{2,1,0:T(8,128)(2,1)} %broadcast_in_dim.21), calls=%async_computation.3 | async-start | bytes 720896 | tf_op jit(solution)/shard_map/all_to_all | solution.py:11
  21.5 3.2 %abs_reduce_fusion.1 = bf16[8,1408]{1,0:T(8,128)(2,1)S(1)} fusion(f32[8,128,1408]{2,1,0:T(8,128)} %param.6), kind=kLoop, calls=%fused_computation.4 | loop fusion | flops 2872320 | bytes 5789696 | tf_op jit(solution)/shard_map/reduce_sum | solution.py:71
  24.8 4.1 %all-to-all-done.3 = bf16[16,8,1408]{2,1,0:T(8,128)(2,1)S(1)} async-done(((bf16[16,8,1408]{2,1,0:T(8,128)(2,1)}), bf16[16,8,1408]{2,1,0:T(8,128)(2,1)S(1)}, u32[]{:S(2)}, u32[]{:S(2)}) %all-to-all-start.3) | async-done | bytes 360480 | tf_op jit(solution)/shard_map/all_to_all | solution.py:11
  28.9 0.7 broadcast_in_dim.23
  29.6 5.3 %all-to-all-start.7 = ((bf16[8,2048,8]{1,2,0:T(8,128)(2,1)}), bf16[8,2048,8]{1,2,0:T(8,128)(2,1)S(1)}, u32[]{:S(2)}, u32[]{:S(2)}) async-start(bf16[8,2048,8]{1,2,0:T(8,128)(2,1)} %broadcast_in_dim.23), calls=%async_computation.7 | async-start | bytes 524288 | tf_op jit(solution)/shard_map/all_to_all | solution.py:11
  35.0 3.2 %abs_reduce_fusion.2 = bf16[8,1408]{1,0:T(8,128)(2,1)S(1)} fusion(f32[8,128,1408]{2,1,0:T(8,128)} %param.5), kind=kLoop, calls=%fused_computation.6 | loop fusion | flops 2872320 | bytes 5789696 | tf_op jit(solution)/shard_map/reduce_sum | solution.py:68
  38.2 0.1 convert_reduce_fusion
  38.2 4.2 %all-to-all-done.7 = bf16[8,2048,8]{1,2,0:T(8,128)(2,1)S(1)} async-done(((bf16[8,2048,8]{1,2,0:T(8,128)(2,1)}), bf16[8,2048,8]{1,2,0:T(8,128)(2,1)S(1)}, u32[]{:S(2)}, u32[]{:S(2)}) %all-to-all-start.7) | async-done | bytes 262176 | tf_op jit(solution)/shard_map/all_to_all | solution.py:11
  42.5 0.8 broadcast_in_dim.20
  43.2 5.3 %all-to-all-start.1 = ((bf16[16,8,1408]{2,1,0:T(8,128)(2,1)}), bf16[16,8,1408]{2,1,0:T(8,128)(2,1)S(1)}, u32[]{:S(2)}, u32[]{:S(2)}) async-start(bf16[16,8,1408]{2,1,0:T(8,128)(2,1)} %broadcast_in_dim.20), calls=%async_computation.1 | async-start | bytes 720896 | tf_op jit(solution)/shard_map/all_to_all | solution.py:11
  48.5 7.6 %all-to-all-done.1 = bf16[16,8,1408]{2,1,0:T(8,128)(2,1)S(1)} async-done(((bf16[16,8,1408]{2,1,0:T(8,128)(2,1)}), bf16[16,8,1408]{2,1,0:T(8,128)(2,1)S(1)}, u32[]{:S(2)}, u32[]{:S(2)}) %all-to-all-start.1) | async-done | bytes 360480 | tf_op jit(solution)/shard_map/all_to_all | solution.py:11
  56.2 0.8 broadcast_in_dim.19
  56.9 6.1 %all-to-all-start = ((bf16[16,8,1408]{2,1,0:T(8,128)(2,1)}), bf16[16,8,1408]{2,1,0:T(8,128)(2,1)}, u32[]{:S(2)}, u32[]{:S(2)}) async-start(bf16[16,8,1408]{2,1,0:T(8,128)(2,1)} %broadcast_in_dim.19), calls=%async_computation | async-start | bytes 720896 | tf_op jit(solution)/shard_map/all_to_all | solution.py:11
  63.1 4.2 %divide_convert_fusion = bf16[8,1408,128]{2,1,0:T(8,128)(2,1)S(1)} fusion(f32[8,1408,128]{2,1,0:T(8,128)} %param.7, f32[8,1408]{1,0:T(8,128)S(1)} %broadcast_multiply_fusion), kind=kLoop, calls=%fused_computation.1 | loop fusion | flops 2883584 | bytes 8695808 | tf_op jit(solution)/shard_map/convert_element_type | solution.py:84
  67.3 0.1 split.24
  67.4 1.2 copy.46
  68.7 1.7 all-to-all-done
  70.4 6.3 %all-to-all-start.4 = ((bf16[16,8,40,128]{3,2,1,0:T(8,128)(2,1)}), bf16[16,8,40,128]{3,2,1,0:T(8,128)(2,1)}, u32[]{:S(2)}, u32[]{:S(2)}) async-start(bf16[16,8,40,128]{3,2,1,0:T(8,128)(2,1)} %copy.46), calls=%async_computation.4 | async-start | bytes 2621440 | tf_op jit(solution)/shard_map/all_to_all | solution.py:58
  76.7 6.5 %copy.40 = f32[8,128,1408]{1,0,2:T(8,128)} copy(f32[8,128,1408]{2,1,0:T(8,128)} %param.5) | data formatting | bytes 11534336 | tf_op args[0]
  83.2 6.5 %copy.42 = f32[8,128,1408]{1,0,2:T(8,128)} copy(f32[8,128,1408]{2,1,0:T(8,128)} %param.6) | data formatting | bytes 11534336 | tf_op args[1]
  89.6 1.3 split.25
  90.9 1.0 convert_reduce_fusion.2
  91.9 0.0 copy-start
  92.0 0.3 copy.39
  92.2 0.1 convert_reduce_fusion.1
  92.3 0.3 copy-done
  92.6 0.3 copy.41
  92.8 2.7 %copy.47 = bf16[16,8,48,128]{3,2,1,0:T(8,128)(2,1)} copy(bf16[16,8,48,128]{3,2,0,1:T(8,128)(2,1)} %split.25) | data formatting | bytes 3145728 | tf_op jit(solution)/shard_map/split | solution.py:56
  95.6 0.0 all-to-all-done.4
  95.6 7.3 %all-to-all-start.5 = ((bf16[16,8,48,128]{3,2,1,0:T(8,128)(2,1)}), bf16[16,8,48,128]{3,2,1,0:T(8,128)(2,1)S(1)}, u32[]{:S(2)}, u32[]{:S(2)}) async-start(bf16[16,8,48,128]{3,2,1,0:T(8,128)(2,1)} %copy.47), calls=%async_computation.5 | async-start | bytes 3145728 | tf_op jit(solution)/shard_map/all_to_all | solution.py:58
  102.8 6.4 %divide_convert_fusion.1 = (bf16[8,128,1408]{1,0,2:T(8,128)(2,1)S(1)}, bf16[8,128,1408]{1,0,2:T(8,128)(2,1)S(1)}) fusion(f32[8,128,1408]{1,0,2:T(8,128)} %copy.42, f32[8,1408]{0,1:T(8,128)S(1)} %copy.41, f32[8,128,1408]{1,0,2:T(8,128)} %copy.40, f32[8,1408]{0,1:T(8,128)S(1)} %copy.39), kind=kLoop, calls=%fused_computation.3 | loop fusion | flops 5767168 | bytes 17391616 | tf_op jit(solution)/shard_map/convert_element_type | solution.py:83
  109.2 3.3 %pad_maximum_fusion = bf16[16,128,1408]{1,0,2:T(8,128)(2,1)} fusion(bf16[8,128,1408]{1,0,2:T(8,128)(2,1)S(1)} %get-tuple-element.9, bf16[8,128,1408]{1,0,2:T(8,128)(2,1)S(1)} %get-tuple-element.10), kind=kLoop, calls=%fused_computation | loop fusion | flops 11534336 | bytes 11534336 | tf_op jit(solution)/shard_map/concatenate | solution.py:24
  112.4 8.9 %all-to-all-done.5 = bf16[16,8,48,128]{3,2,1,0:T(8,128)(2,1)S(1)} async-done(((bf16[16,8,48,128]{3,2,1,0:T(8,128)(2,1)}), bf16[16,8,48,128]{3,2,1,0:T(8,128)(2,1)S(1)}, u32[]{:S(2)}, u32[]{:S(2)}) %all-to-all-start.5) | async-done | bytes 1572896 | tf_op jit(solution)/shard_map/all_to_all | solution.py:58
  121.4 7.4 %all-to-all-start.2 = ((bf16[16,128,1408]{1,0,2:T(8,128)(2,1)}), bf16[16,128,1408]{1,0,2:T(8,128)(2,1)}, u32[]{:S(2)}, u32[]{:S(2)}) async-start(bf16[16,128,1408]{1,0,2:T(8,128)(2,1)} %pad_maximum_fusion), calls=%async_computation.2 | async-start | bytes 11534336 | tf_op jit(solution)/shard_map/all_to_all | solution.py:27
  128.8 0.7 constant_dynamic-slice_fusion
  129.4 0.7 constant_dynamic-slice_fusion.1
  130.1 1.4 constant_dynamic-slice_fusion.2
  131.5 3.3 %copy_bitcast_fusion = bf16[8,88,2048]{2,1,0:T(8,128)(2,1)} fusion(bf16[16,8,48,128]{3,2,1,0:T(8,128)(2,1)S(1)} %all-to-all-done.5, bf16[16,8,40,128]{3,2,1,0:T(8,128)(2,1)} %all-to-all-done.4), kind=kLoop, calls=%fused_computation.7 | loop fusion | flops 5767168 | bytes 5767168 | tf_op jit(solution)/shard_map/reshape | solution.py:49
  134.8 72.1 %all-to-all-done.2 = bf16[16,128,1408]{1,0,2:T(8,128)(2,1)} async-done(((bf16[16,128,1408]{1,0,2:T(8,128)(2,1)}), bf16[16,128,1408]{1,0,2:T(8,128)(2,1)}, u32[]{:S(2)}, u32[]{:S(2)}) %all-to-all-start.2) | async-done | bytes 5767200 | tf_op jit(solution)/shard_map/all_to_all | solution.py:27
  206.9 4.1 %copy.43 = bf16[16,128,1408]{1,2,0:T(8,128)(2,1)S(1)} copy(bf16[16,128,1408]{1,0,2:T(8,128)(2,1)} %all-to-all-done.2) | data formatting | bytes 11534336 | tf_op jit(solution)/shard_map/all_to_all | solution.py:27
  211.0 1.0 slice_bitcast_fusion
  212.0 2.4 %copy.55 = bf16[8,16,11,8,128]{4,3,1,2,0:T(8,128)(2,1)} copy(bf16[8,16,11,8,128]{4,3,2,1,0:T(8,128)(2,1)S(1)} %get-tuple-element.7) | data formatting | bytes 5767168 | tf_op jit(solution)/shard_map/split | solution.py:26
  214.4 2.4 %copy.56 = bf16[8,16,11,8,128]{4,3,1,2,0:T(8,128)(2,1)} copy(bf16[8,16,11,8,128]{4,3,2,1,0:T(8,128)(2,1)S(1)} %get-tuple-element.8) | data formatting | bytes 5767168 | tf_op jit(solution)/shard_map/split | solution.py:26
  216.7 0.7 copy.58
  (3 shorter events, 0.0 us)
Async XLA Ops:
  1.9 13.6 %all-to-all-start.6 = ((bf16[16,128,8]{1,2,0:T(8,128)(2,1)}), bf16[16,128,8]{1,2,0:T(8,128)(2,1)S(1)}, u32[]{:S(2)}, u32[]{:S(2)}) async-start(bf16[16,128,8]{1,2,0:T(8,128)(2,1)} %broadcast_in_dim.22), calls=%async_computation.6 | async-start | bytes 65536 | tf_op jit(solution)/shard_map/all_to_all | solution.py:11
  16.3 12.6 %all-to-all-start.3 = ((bf16[16,8,1408]{2,1,0:T(8,128)(2,1)}), bf16[16,8,1408]{2,1,0:T(8,128)(2,1)S(1)}, u32[]{:S(2)}, u32[]{:S(2)}) async-start(bf16[16,8,1408]{2,1,0:T(8,128)(2,1)} %broadcast_in_dim.21), calls=%async_computation.3 | async-start | bytes 720896 | tf_op jit(solution)/shard_map/all_to_all | solution.py:11
  29.6 12.8 %all-to-all-start.7 = ((bf16[8,2048,8]{1,2,0:T(8,128)(2,1)}), bf16[8,2048,8]{1,2,0:T(8,128)(2,1)S(1)}, u32[]{:S(2)}, u32[]{:S(2)}) async-start(bf16[8,2048,8]{1,2,0:T(8,128)(2,1)} %broadcast_in_dim.23), calls=%async_computation.7 | async-start | bytes 524288 | tf_op jit(solution)/shard_map/all_to_all | solution.py:11
  43.2 12.9 %all-to-all-start.1 = ((bf16[16,8,1408]{2,1,0:T(8,128)(2,1)}), bf16[16,8,1408]{2,1,0:T(8,128)(2,1)S(1)}, u32[]{:S(2)}, u32[]{:S(2)}) async-start(bf16[16,8,1408]{2,1,0:T(8,128)(2,1)} %broadcast_in_dim.20), calls=%async_computation.1 | async-start | bytes 720896 | tf_op jit(solution)/shard_map/all_to_all | solution.py:11
  56.9 13.4 %all-to-all-start = ((bf16[16,8,1408]{2,1,0:T(8,128)(2,1)}), bf16[16,8,1408]{2,1,0:T(8,128)(2,1)}, u32[]{:S(2)}, u32[]{:S(2)}) async-start(bf16[16,8,1408]{2,1,0:T(8,128)(2,1)} %broadcast_in_dim.19), calls=%async_computation | async-start | bytes 720896 | tf_op jit(solution)/shard_map/all_to_all | solution.py:11
  70.4 25.2 %all-to-all-start.4 = ((bf16[16,8,40,128]{3,2,1,0:T(8,128)(2,1)}), bf16[16,8,40,128]{3,2,1,0:T(8,128)(2,1)}, u32[]{:S(2)}, u32[]{:S(2)}) async-start(bf16[16,8,40,128]{3,2,1,0:T(8,128)(2,1)} %copy.46), calls=%async_computation.4 | async-start | bytes 2621440 | tf_op jit(solution)/shard_map/all_to_all | solution.py:58
  91.9 0.6 copy-start
  95.6 25.8 %all-to-all-start.5 = ((bf16[16,8,48,128]{3,2,1,0:T(8,128)(2,1)}), bf16[16,8,48,128]{3,2,1,0:T(8,128)(2,1)S(1)}, u32[]{:S(2)}, u32[]{:S(2)}) async-start(bf16[16,8,48,128]{3,2,1,0:T(8,128)(2,1)} %copy.47), calls=%async_computation.5 | async-start | bytes 3145728 | tf_op jit(solution)/shard_map/all_to_all | solution.py:58
  121.4 85.5 %all-to-all-start.2 = ((bf16[16,128,1408]{1,0,2:T(8,128)(2,1)}), bf16[16,128,1408]{1,0,2:T(8,128)(2,1)}, u32[]{:S(2)}, u32[]{:S(2)}) async-start(bf16[16,128,1408]{1,0,2:T(8,128)(2,1)} %pad_maximum_fusion), calls=%async_computation.2 | async-start | bytes 11534336 | tf_op jit(solution)/shard_map/all_to_all | solution.py:27
where the time goes:
time: 219 us; the launch traced here: 217 us
  waiting for transfers between devices  101 us (46%)
  starting transfers between devices  50.3 us (23%)
  local copies, waits for them, and re-layouts  36 us (16%)
  other arithmetic  29.7 us (14%)
    all_to_all x1, waiting for transfers between devices, in_one_piece(): lax.all_to_all(both, axis, split_axis=split_dim, concat_axis=concat_dim,...  72.1 us
    all_to_all x5, starting transfers between devices, sent_to_all(): return lax.all_to_all(copies, axis, split_axis=0, concat_axis=0, tiled=True)  29.3 us
    all_to_all x5, waiting for transfers between devices, sent_to_all(): return lax.all_to_all(copies, axis, split_axis=0, concat_axis=0, tiled=True)  19.7 us
    unnamed x6, local copies, waits for them, and re-layouts  14.9 us
    all_to_all x2, starting transfers between devices, exchange_in_pieces(): lax.all_to_all(section, axis, split_axis=0, concat_axis=0, tiled=True)  13.6 us
    all_to_all x2, waiting for transfers between devices, exchange_in_pieces(): lax.all_to_all(section, axis, split_axis=0, concat_axis=0, tiled=True)  8.95 us
    all_to_all x1, starting transfers between devices, in_one_piece(): lax.all_to_all(both, axis, split_axis=split_dim, concat_axis=concat_dim,...  7.36 us
    convert_element_type x1, other arithmetic, shards(): (train_up / jnp.expand_dims(scale_up, 1)).astype(jnp.bfloat16)  6.35 us
  transfers between devices with their start and end apart: 8, of which 7 were waited for; matrix products, arithmetic and copies ran while one was open for 23% of the time, Pallas kernels for 0%

commit v1 on v0

v1 whole, which is shorter than its diff:
```python
import jax
import jax.numpy as jnp
from jax import lax
from jax.experimental import pallas as pl
from jax.experimental.pallas import tpu as pltpu
from jax.sharding import PartitionSpec as P

D_MODEL = 2048
PEERS = 16
OWN = 8
COLS = 88
LANES = 128


def pack_down_kernel(down, router, gain, out):
    step = pl.program_id(0)

    @pl.when(step < OWN)
    def _():
        for peer in range(PEERS):
            out[peer] = down[0, COLS * peer : COLS * (peer + 1), :].astype(jnp.bfloat16)

    @pl.when(step == OWN)
    def _():
        served = (router[...] * gain[...]).astype(jnp.bfloat16)
        for peer in range(PEERS):
            out[peer, 0:OWN, :] = served


def pack_down(down, router, gain):
    return pl.pallas_call(
        pack_down_kernel,
        grid=(OWN + 1,),
        in_specs=[
            pl.BlockSpec((1, PEERS * COLS, LANES), lambda e: (jnp.minimum(e, OWN - 1), 0, 0)),
            pl.BlockSpec((OWN, LANES), lambda e: (0, 0)),
            pl.BlockSpec((1, LANES), lambda e: (0, 0)),
        ],
        out_specs=pl.BlockSpec((PEERS, COLS, LANES), lambda e: (0, e, 0)),
        out_shape=jax.ShapeDtypeStruct((PEERS, OWN * COLS + OWN, LANES), jnp.bfloat16),
        name="pack_down",
    )(down, router, gain)


def pack_columns_kernel(gate, up, out):
    for which, ref in enumerate((gate, up)):
        turned = ref[0].astype(jnp.bfloat16).T
        for peer in range(PEERS):
            out[peer, which, 0] = turned[COLS * peer : COLS * (peer + 1), :]


def pack_columns(gate, up):
    block = pl.BlockSpec((1, LANES, PEERS * COLS), lambda e: (e, 0, 0))
    return pl.pallas_call(
        pack_columns_kernel,
        grid=(OWN,),
        in_specs=[block, block],
        out_specs=pl.BlockSpec((PEERS, 2, 1, COLS, LANES), lambda e: (0, 0, e, 0, 0)),
        out_shape=jax.ShapeDtypeStruct((PEERS, 2, OWN, COLS, LANES), jnp.bfloat16),
        name="pack_columns",
    )(gate, up)


def finish(total_of, ready, scales, step):
    total = jnp.zeros((COLS, LANES), jnp.float32)
    for peer in range(PEERS):
        total = total + jnp.abs(total_of(peer).astype(jnp.float32))
    factor = D_MODEL / jnp.sum(total, axis=1, keepdims=True)
    scales[pl.ds(step, 1), :] = jnp.sum(total.T, axis=0, keepdims=True) / D_MODEL
    for peer in range(PEERS):
        ready[0, :, LANES * peer : LANES * (peer + 1)] = (
            total_of(peer).astype(jnp.float32) * factor
        ).astype(jnp.bfloat16)


def finish_down_kernel(got, ready, scales):
    finish(lambda peer: got[peer], ready, scales, pl.program_id(0))


def finish_columns_kernel(got, ready_gate, ready_up, scales_gate, scales_up):
    step = pl.program_id(0)
    finish(lambda peer: got[peer, 0, 0], ready_gate, scales_gate, step)
    finish(lambda peer: got[peer, 1, 0], ready_up, scales_up, step)


READY = jax.ShapeDtypeStruct((OWN, COLS, D_MODEL), jnp.bfloat16)
SCALE = jax.ShapeDtypeStruct((OWN, COLS), jnp.float32)
READY_BLOCK = pl.BlockSpec((1, COLS, D_MODEL), lambda e: (e, 0, 0))
SCALE_BLOCK = pl.BlockSpec((OWN, COLS), lambda e: (0, 0))


def finish_down(got):
    return pl.pallas_call(
        finish_down_kernel,
        grid=(OWN,),
        in_specs=[pl.BlockSpec((PEERS, COLS, LANES), lambda e: (0, e, 0))],
        out_specs=[READY_BLOCK, SCALE_BLOCK],
        out_shape=[READY, SCALE],
        name="finish_down",
    )(got)


def finish_columns(got):
    return pl.pallas_call(
        finish_columns_kernel,
        grid=(OWN,),
        in_specs=[pl.BlockSpec((PEERS, 2, 1, COLS, LANES), lambda e: (0, 0, e, 0, 0))],
        out_specs=[READY_BLOCK, READY_BLOCK, SCALE_BLOCK, SCALE_BLOCK],
        out_shape=[READY, READY, SCALE, SCALE],
        name="finish_columns",
    )(got)


def to_owners(parts):
    return lax.all_to_all(parts, "fsdp", split_axis=0, concat_axis=0, tiled=True)


def shards(train_gate, train_up, train_down, router_weight, router_gain):
    got_down = to_owners(
        pack_down(train_down, jnp.swapaxes(router_weight, 0, 1), router_gain[None, :])
    )
    got_columns = to_owners(pack_columns(train_gate, train_up))
    rows = jnp.swapaxes(got_down[:, OWN * COLS :, :], 0, 1).reshape(OWN, D_MODEL)
    serve_router = lax.all_gather(rows, "ep", axis=0, tiled=True)
    ready_down, scale_down = finish_down(got_down)
    ready_gate, ready_up, scale_gate, scale_up = finish_columns(got_columns)
    return (
        jnp.swapaxes(ready_gate, 1, 2),
        jnp.swapaxes(ready_up, 1, 2),
        ready_down,
        scale_gate,
        scale_up,
        scale_down,
        jnp.swapaxes(serve_router, 0, 1),
    )


def solution(mesh):
    in_specs = (
        P("ep", "fsdp", None),
        P("ep", "fsdp", None),
        P("ep", None, "fsdp"),
        P("fsdp", "ep"),
        P("fsdp"),
    )
    out_specs = (
        P("ep", None, "fsdp"),
        P("ep", None, "fsdp"),
        P("ep", "fsdp", None),
        P("ep", "fsdp"),
        P("ep", "fsdp"),
        P("ep", "fsdp"),
        P(),
    )
    return jax.shard_map(shards, mesh=mesh, in_specs=in_specs, out_specs=out_specs, check_vma=False)
```

time: 219 us -> 158 us (0.72)
  starting transfers between devices: 50.3 us -> 13.7 us
  local copies, waits for them, and re-layouts: 36 us -> 0.71 us
  Pallas kernels: 0 us -> 31.2 us
  other arithmetic: 29.7 us -> 0 us
  blocking collectives: 0 us -> 14 us
  waiting for transfers between devices: 101 us -> 95.5 us
    all_to_all x8 -> x2, starting transfers between devices: 50.3 us -> 13.7 us  [to_owners(): lax.all_to_all(parts, 'fsdp', split_axis=0, concat_axis=0, tiled=True)]
    pallas_call x0 -> x4, Pallas kernels: none -> 31.2 us  [the longest x1 9.39 us: pack_columns(): pl.pallas_call(pack_columns_kernel, grid=(OWN,), in_specs=[block, block],...]
    unnamed x6 -> x3, local copies, waits for them, and re-layouts: 14.9 us -> 0.71 us
    all_gather x0 -> x1, blocking collectives: none -> 14 us  [shards(): serve_router = lax.all_gather(rows, 'ep', axis=0, tiled=True)]
    reduce_sum x6 -> x0, other arithmetic: 11.8 us -> none  [the longest x1 4.2 us: shards(): jnp.sum(jnp.abs(train_down), axis=2).astype(jnp.bfloat16)]
    convert_element_type x3 -> x0, other arithmetic: 11.3 us -> none  [the longest x1 6.35 us: shards(): (train_up / jnp.expand_dims(scale_up, 1)).astype(jnp.bfloat16)]
    split x6 -> x0, local copies, waits for them, and re-layouts: 10.1 us -> none  [the longest x4 5.34 us: exchange_in_pieces(): jnp.split(parts, edges_of(parts.shape[split_at], pieces), axis=split_at)]
    all_to_all x8 -> x2, waiting for transfers between devices: 101 us -> 95.5 us  [to_owners(): lax.all_to_all(parts, 'fsdp', split_axis=0, concat_axis=0, tiled=True)]
  transfers between devices with their start and end apart: 8 -> 2, of which waited for: 7 -> 2; matrix products, arithmetic and copies ran while one was open for 23% -> 0% of each run, Pallas kernels for 0% -> 10%
where the time goes in v1:
time: 158 us; the launch traced here: 156 us
  waiting for transfers between devices  95.5 us (60%)
  Pallas kernels  31.2 us (20%)
  blocking collectives  14 us (9%)
  starting transfers between devices  13.7 us (9%)
    all_to_all x2, waiting for transfers between devices, to_owners(): lax.all_to_all(parts, 'fsdp', split_axis=0, concat_axis=0, tiled=True)  95.5 us
    all_gather x1, blocking collectives, shards(): serve_router = lax.all_gather(rows, 'ep', axis=0, tiled=True)  14 us
    all_to_all x2, starting transfers between devices, to_owners(): lax.all_to_all(parts, 'fsdp', split_axis=0, concat_axis=0, tiled=True)  13.7 us
    pallas_call x1, Pallas kernels, pack_columns(): pl.pallas_call(pack_columns_kernel, grid=(OWN,), in_specs=[block, block],...  9.39 us
    pallas_call x1, Pallas kernels, finish_columns(): pl.pallas_call(finish_columns_kernel, grid=(OWN,), in_specs=[pl.BlockSpec...  8.44 us
    pallas_call x1, Pallas kernels, pack_down(): pl.pallas_call(pack_down_kernel, grid=(OWN + 1,), in_specs=[pl.BlockSpec(...  6.77 us
    pallas_call x1, Pallas kernels, finish_down(): pl.pallas_call(finish_down_kernel, grid=(OWN,), in_specs=[pl.BlockSpec((P...  6.57 us
  transfers between devices with their start and end apart: 2, of which 2 were waited for; matrix products, arithmetic and copies ran while one was open for 0% of the time, Pallas kernels for 10%

profile of v1, /device:TPU:8, one launch (start us, length us, event | category | flops | bytes accessed | tf_op | source)
XLA Modules:
  0.0 155.8 jit_solution(13189932705129330126)
XLA Ops:
  0.6 6.8 %pack_down.1 = bf16[16,712,128]{2,1,0:T(8,128)(2,1)} custom-call(f32[8,1408,128]{2,1,0:T(8,128)} %down.1, f32[8,128]{1,0:T(8,128)} %bitcast.10, f32[1,128]{1,0:T(1,128)} %bitcast.11), custom_call_target="tpu_custom_call" | custom-call | tf_op jit(solution)/shard_map/pack_down/pallas_call | solution.py:31
  7.4 7.4 %all-to-all-start.1 = ((bf16[16,712,128]{2,1,0:T(8,128)(2,1)}), bf16[16,712,128]{2,1,0:T(8,128)(2,1)S(1)}, u32[]{:S(2)}, u32[]{:S(2)}) async-start(bf16[16,712,128]{2,1,0:T(8,128)(2,1)} %pack_down.1), calls=%async_computation.1 | async-start | bytes 5832704 | tf_op jit(solution)/shard_map/all_to_all | solution.py:115
  14.8 9.4 %pack_columns.1 = bf16[16,2,8,88,128]{4,3,2,1,0:T(8,128)(2,1)} custom-call(f32[8,128,1408]{2,1,0:T(8,128)} %gate.1, f32[8,128,1408]{2,1,0:T(8,128)} %up.1), custom_call_target="tpu_custom_call" | custom-call | tf_op jit(solution)/shard_map/pack_columns/pallas_call | solution.py:54
  24.2 33.0 %all-to-all-done.1.got = bf16[16,712,128]{2,1,0:T(8,128)(2,1)S(1)} async-done(((bf16[16,712,128]{2,1,0:T(8,128)(2,1)}), bf16[16,712,128]{2,1,0:T(8,128)(2,1)S(1)}, u32[]{:S(2)}, u32[]{:S(2)}) %all-to-all-start.1) | async-done | bytes 2916384 | tf_op jit(solution)/shard_map/all_to_all | solution.py:115
  57.2 0.0 copy-start
  57.2 6.3 %all-to-all-start = ((bf16[16,2,8,88,128]{4,3,2,1,0:T(8,128)(2,1)}), bf16[16,2,8,88,128]{4,3,2,1,0:T(8,128)(2,1)}, u32[]{:S(2)}, u32[]{:S(2)}) async-start(bf16[16,2,8,88,128]{4,3,2,1,0:T(8,128)(2,1)} %pack_columns.1), calls=%async_computation | async-start | bytes 11534336 | tf_op jit(solution)/shard_map/all_to_all | solution.py:115
  63.5 0.0 copy-done
  63.5 14.0 %all_gather.3 = bf16[64,2048]{1,0:T(8,128)(2,1)S(1)} all-gather(bf16[8,2048]{1,0:T(8,128)(2,1)S(1)} %slice_bitcast_fusion), channel_id=1, replica_groups=mesh['ep'=8,'fsdp'=16] {'ep'}, dimensions={0}, use_global_device_ids=true | all-gather | bytes 294912 | tf_op jit(solution)/shard_map/all_gather | solution.py:124
  77.5 6.6 %finish_down.1 = (bf16[8,88,2048]{2,1,0:T(8,128)(2,1)}, f32[8,88]{1,0:T(8,128)}) custom-call(bf16[16,712,128]{2,1,0:T(8,128)(2,1)} %copy-done), custom_call_target="tpu_custom_call" | custom-call | tf_op jit(solution)/shard_map/finish_down/pallas_call | solution.py:93
  84.1 62.5 %all-to-all-done.got = bf16[16,2,8,88,128]{4,3,2,1,0:T(8,128)(2,1)} async-done(((bf16[16,2,8,88,128]{4,3,2,1,0:T(8,128)(2,1)}), bf16[16,2,8,88,128]{4,3,2,1,0:T(8,128)(2,1)}, u32[]{:S(2)}, u32[]{:S(2)}) %all-to-all-start) | async-done | bytes 5767200 | tf_op jit(solution)/shard_map/all_to_all | solution.py:115
  146.6 8.4 %finish_columns.1 = (bf16[8,88,2048]{2,1,0:T(8,128)(2,1)}, bf16[8,88,2048]{2,1,0:T(8,128)(2,1)}, f32[8,88]{1,0:T(8,128)}, f32[8,88]{1,0:T(8,128)}) custom-call(bf16[16,2,8,88,128]{4,3,2,1,0:T(8,128)(2,1)} %all-to-all-done.got), custom_call_target="tpu_custom_call" | custom-call | tf_op jit(solution)/shard_map/finish_columns/pallas_call | solution.py:104
  155.1 0.7 copy.13
  (1 shorter events, 0.0 us)
Async XLA Ops:
  7.4 49.8 %all-to-all-start.1 = ((bf16[16,712,128]{2,1,0:T(8,128)(2,1)}), bf16[16,712,128]{2,1,0:T(8,128)(2,1)S(1)}, u32[]{:S(2)}, u32[]{:S(2)}) async-start(bf16[16,712,128]{2,1,0:T(8,128)(2,1)} %pack_down.1), calls=%async_computation.1 | async-start | bytes 5832704 | tf_op jit(solution)/shard_map/all_to_all | solution.py:115
  57.2 6.3 %copy-start = (bf16[16,712,128]{2,1,0:T(8,128)(2,1)}, bf16[16,712,128]{2,1,0:T(8,128)(2,1)S(1)}, u32[]{:S(2)}) copy-start(bf16[16,712,128]{2,1,0:T(8,128)(2,1)S(1)} %all-to-all-done.1.got) | copy-start | bytes 8749060
  57.2 89.5 %all-to-all-start = ((bf16[16,2,8,88,128]{4,3,2,1,0:T(8,128)(2,1)}), bf16[16,2,8,88,128]{4,3,2,1,0:T(8,128)(2,1)}, u32[]{:S(2)}, u32[]{:S(2)}) async-start(bf16[16,2,8,88,128]{4,3,2,1,0:T(8,128)(2,1)} %pack_columns.1), calls=%async_computation | async-start | bytes 11534336 | tf_op jit(solution)/shard_map/all_to_all | solution.py:115

commit v2 on v1

v2 whole, which is shorter than its diff:
```python
import jax
import jax.numpy as jnp
from jax import lax
from jax.experimental import pallas as pl
from jax.experimental.pallas import tpu as pltpu
from jax.sharding import PartitionSpec as P

D_MODEL = 2048
SIDE = 4
PEERS = 16
OWN = 8
COLS = 88
LANES = 128
ROWS = OWN * COLS
FIRST_ROWS = 2 * ROWS + OWN

HOPS = (
    (1, 1), (3, 3),
    (3, 1), (1, 3),
    (0, 2), (2, 0),
    (2, 2),
    (1, 2), (3, 0),
    (3, 2), (1, 0),
    (2, 1), (0, 3),
    (2, 3), (0, 1),
)
HBM = pl.BlockSpec(memory_space=pltpu.HBM)
ANY = pl.BlockSpec(memory_space=pl.ANY)
VMEM = pl.BlockSpec(memory_space=pltpu.VMEM)
SMEM = pl.BlockSpec(memory_space=pltpu.SMEM)


def moved(me, hop, sign):
    y, x = me // SIDE, me % SIDE
    return (y + SIDE + sign * hop[0]) % SIDE * SIDE + (x + SIDE + sign * hop[1]) % SIDE


def started(copies):
    for copy in copies:
        copy.start()
    return copies


def send_out(me, packed, outs, sems):
    copies = started(
        [
            pltpu.make_async_copy(packed.at[moved(me, hop, 1)], out, sems.at[k])
            for k, (hop, out) in enumerate(zip(((0, 0), *HOPS), outs))
        ]
    )
    for copy in copies:
        copy.wait()


def turned_in(raw, packed, base):
    turned = raw[...].astype(jnp.bfloat16).T
    for peer in range(PEERS):
        packed[peer, base : base + COLS, :] = turned[COLS * peer : COLS * (peer + 1), :]


def pack_first_kernel(me, gate, down, router, gain, *rest):
    outs, (raw_gate, raw_down, packed, sems_gate, sems_down, sems_out) = rest[:PEERS], rest[PEERS:]
    gates = [pltpu.make_async_copy(gate.at[e], raw_gate.at[e], sems_gate.at[e]) for e in range(OWN)]
    downs = [pltpu.make_async_copy(down.at[e], raw_down.at[e], sems_down.at[e]) for e in range(OWN)]
    for e in range(OWN):
        gates[e].start()
        downs[e].start()
    served = (router[...] * gain[...]).astype(jnp.bfloat16)
    for peer in range(PEERS):
        packed[peer, 2 * ROWS :, :] = served
    for e in range(OWN):
        gates[e].wait()
        turned_in(raw_gate.at[e], packed, ROWS + COLS * e)
        downs[e].wait()
        for peer in range(PEERS):
            packed[peer, COLS * e : COLS * (e + 1), :] = raw_down[
                e, COLS * peer : COLS * (peer + 1), :
            ].astype(jnp.bfloat16)
    send_out(me[0], packed, outs, sems_out)


def pack_first(me, gate, down, router, gain):
    return pl.pallas_call(
        pack_first_kernel,
        in_specs=[SMEM, HBM, HBM, VMEM, VMEM],
        out_specs=[ANY] * PEERS,
        out_shape=[jax.ShapeDtypeStruct((FIRST_ROWS, LANES), jnp.bfloat16)] * PEERS,
        scratch_shapes=[
            pltpu.VMEM((OWN, LANES, PEERS * COLS), jnp.float32),
            pltpu.VMEM((OWN, PEERS * COLS, LANES), jnp.float32),
            pltpu.VMEM((PEERS, FIRST_ROWS, LANES), jnp.bfloat16),
            pltpu.SemaphoreType.DMA((OWN,)),
            pltpu.SemaphoreType.DMA((OWN,)),
            pltpu.SemaphoreType.DMA((PEERS,)),
        ],
        compiler_params=pltpu.CompilerParams(vmem_limit_bytes=59 << 20),
        name="pack_first",
    )(me, gate, down, router, gain)


def pack_last_kernel(me, up, _, *rest):
    outs, (raw, packed, sems_in, sems_out) = rest[:PEERS], rest[PEERS:]
    copies = started(
        [pltpu.make_async_copy(up.at[e], raw.at[e], sems_in.at[e]) for e in range(OWN)]
    )
    for e in range(OWN):
        copies[e].wait()
        turned_in(raw.at[e], packed, COLS * e)
    send_out(me[0], packed, outs, sems_out)


def pack_last(me, up, after):
    return pl.pallas_call(
        pack_last_kernel,
        in_specs=[SMEM, HBM, ANY],
        out_specs=[ANY] * PEERS,
        out_shape=[jax.ShapeDtypeStruct((ROWS, LANES), jnp.bfloat16)] * PEERS,
        scratch_shapes=[
            pltpu.VMEM((OWN, LANES, PEERS * COLS), jnp.float32),
            pltpu.VMEM((PEERS, ROWS, LANES), jnp.bfloat16),
            pltpu.SemaphoreType.DMA((OWN,)),
            pltpu.SemaphoreType.DMA((PEERS,)),
        ],
        compiler_params=pltpu.CompilerParams(vmem_limit_bytes=10 << 20),
        name="pack_last",
    )(me, up, after)


def finish(got, made, q, e, scales):
    rows = slice(COLS * q, COLS * (q + 1))
    total = jnp.abs(got[0, rows, :].astype(jnp.float32))
    for peer in range(1, PEERS):
        total = total + jnp.abs(got[peer, rows, :].astype(jnp.float32))
    factor = D_MODEL / jnp.sum(total, axis=1, keepdims=True)
    scales[e : e + 1, :] = jnp.sum(total.T, axis=0, keepdims=True) / D_MODEL
    for peer in range(PEERS):
        made[q, :, LANES * peer : LANES * (peer + 1)] = (
            got[peer, rows, :].astype(jnp.float32) * factor
        ).astype(jnp.bfloat16)


def finish_kernel(me, parts, outs, routed, got, made, sems_in, sems_out):
    pair = 2 * COLS
    pairs = len(outs) * OWN // 2
    ranges = [(pair * w, pair) for w in range(pairs)]
    if routed is not None:
        ranges.append((pair * pairs, OWN))
    waves = []
    for wave, (start, size) in enumerate(ranges):
        rows = pl.ds(start, size)
        waves.append(
            started(
                [
                    pltpu.make_async_copy(
                        part.at[rows], got.at[moved(me[0], hop, -1), rows], sems_in.at[wave, k]
                    )
                    for k, (hop, part) in enumerate(zip(((0, 0), *HOPS), parts))
                ]
            )
        )
    writes = []
    for q in range(len(outs) * OWN):
        if q % 2 == 0:
            for copy in waves[q // 2]:
                copy.wait()
        ready, scales = outs[q // OWN]
        finish(got, made, q, q % OWN, scales)
        writes += started(
            [pltpu.make_async_copy(made.at[q], ready.at[q % OWN], sems_out.at[q])]
        )
    if routed is not None:
        for copy in waves[-1]:
            copy.wait()
        for peer in range(PEERS):
            routed[:, LANES * peer : LANES * (peer + 1)] = got[peer, pair * pairs :, :]
    for copy in writes:
        copy.wait()


def finish_first_kernel(me, *rest):
    parts, (down, scale_down, gate, scale_gate, routed, *scratch) = rest[:PEERS], rest[PEERS:]
    got, made, sems_in, sems_out = scratch
    finish_kernel(
        me,
        parts=parts,
        outs=[(down, scale_down), (gate, scale_gate)],
        routed=routed,
        got=got,
        made=made,
        sems_in=sems_in,
        sems_out=sems_out,
    )


def finish_last_kernel(me, _, *rest):
    parts, (up, scale_up, got, made, sems_in, sems_out) = rest[:PEERS], rest[PEERS:]
    finish_kernel(
        me,
        parts=parts,
        outs=[(up, scale_up)],
        routed=None,
        got=got,
        made=made,
        sems_in=sems_in,
        sems_out=sems_out,
    )


READY = jax.ShapeDtypeStruct((OWN, COLS, D_MODEL), jnp.bfloat16)
SCALE = jax.ShapeDtypeStruct((OWN, COLS), jnp.float32)
ROUTED = jax.ShapeDtypeStruct((OWN, D_MODEL), jnp.bfloat16)


def finish_first(me, parts):
    return pl.pallas_call(
        finish_first_kernel,
        in_specs=[SMEM] + [ANY] * PEERS,
        out_specs=[HBM, VMEM, HBM, VMEM, VMEM],
        out_shape=[READY, SCALE, READY, SCALE, ROUTED],
        scratch_shapes=[
            pltpu.VMEM((PEERS, FIRST_ROWS, LANES), jnp.bfloat16),
            pltpu.VMEM((2 * OWN, COLS, D_MODEL), jnp.bfloat16),
            pltpu.SemaphoreType.DMA((OWN + 1, PEERS)),
            pltpu.SemaphoreType.DMA((2 * OWN,)),
        ],
        compiler_params=pltpu.CompilerParams(vmem_limit_bytes=15 << 20),
        name="finish_first",
    )(me, *parts)


def finish_last(me, after, parts):
    return pl.pallas_call(
        finish_last_kernel,
        in_specs=[SMEM, ANY] + [ANY] * PEERS,
        out_specs=[HBM, VMEM],
        out_shape=[READY, SCALE],
        scratch_shapes=[
            pltpu.VMEM((PEERS, ROWS, LANES), jnp.bfloat16),
            pltpu.VMEM((OWN, COLS, D_MODEL), jnp.bfloat16),
            pltpu.SemaphoreType.DMA((OWN // 2, PEERS)),
            pltpu.SemaphoreType.DMA((OWN,)),
        ],
        compiler_params=pltpu.CompilerParams(vmem_limit_bytes=9 << 20),
        name="finish_last",
    )(me, after, *parts)


def to_owners(parts):
    received = [parts[0]]
    for k, hop in enumerate(HOPS):
        route = [(d, moved(d, hop, 1)) for d in range(PEERS)]
        received.append(lax.ppermute(parts[k + 1], "fsdp", route))
    return received


def shards(train_gate, train_up, train_down, router_weight, router_gain):
    me = lax.axis_index("fsdp").astype(jnp.int32)[None]
    router = jnp.swapaxes(router_weight, 0, 1)
    first = pack_first(me, train_gate, train_down, router, router_gain[None, :])
    got_first = to_owners(first)
    last = pack_last(me, train_up, first[0])
    got_last = to_owners(last)
    ready_down, scale_down, ready_gate, scale_gate, routed = finish_first(me, got_first)
    serve_router = lax.all_gather(routed, "ep", axis=0, tiled=True)
    ready_up, scale_up = finish_last(me, serve_router, got_last)
    return (
        jnp.swapaxes(ready_gate, 1, 2),
        jnp.swapaxes(ready_up, 1, 2),
        ready_down,
        scale_gate,
        scale_up,
        scale_down,
        jnp.swapaxes(serve_router, 0, 1),
    )


def solution(mesh):
    in_specs = (
        P("ep", "fsdp", None),
        P("ep", "fsdp", None),
        P("ep", None, "fsdp"),
        P("fsdp", "ep"),
        P("fsdp"),
    )
    out_specs = (
        P("ep", None, "fsdp"),
        P("ep", None, "fsdp"),
        P("ep", "fsdp", None),
        P("ep", "fsdp"),
        P("ep", "fsdp"),
        P("ep", "fsdp"),
        P(),
    )
    return jax.shard_map(shards, mesh=mesh, in_specs=in_specs, out_specs=out_specs, check_vma=False)
```

time: 158 us -> 181 us (1.15)
  the two profiles are of different devices: /device:TPU:8 before, /device:TPU:23 now
where the time goes in v2:
time: 181 us; the launch traced here: 180 us
  starting transfers between devices  61.5 us (34%)
  Pallas kernels  38.3 us (21%)
  waiting for transfers between devices  38 us (21%)
  blocking collectives  37.4 us (21%)
  local copies, waits for them, and re-layouts  4.39 us (2%)
    ppermute x30, starting transfers between devices, to_owners(): received.append(lax.ppermute(parts[k + 1], 'fsdp', route))  61.5 us
    ppermute x30, waiting for transfers between devices, to_owners(): received.append(lax.ppermute(parts[k + 1], 'fsdp', route))  38 us
    all_gather x1, blocking collectives, shards(): serve_router = lax.all_gather(routed, 'ep', axis=0, tiled=True)  37.4 us
    pallas_call x1, Pallas kernels, finish_first(): pl.pallas_call(finish_first_kernel, in_specs=[SMEM] + [ANY] * PEERS, out_...  14.4 us
    pallas_call x1, Pallas kernels, pack_last(): pl.pallas_call(pack_last_kernel, in_specs=[SMEM, HBM, ANY], out_specs=[AN...  8.33 us
    pallas_call x1, Pallas kernels, pack_first(): pl.pallas_call(pack_first_kernel, in_specs=[SMEM, HBM, HBM, VMEM, VMEM],...  7.8 us
    pallas_call x1, Pallas kernels, finish_last(): pl.pallas_call(finish_last_kernel, in_specs=[SMEM, ANY] + [ANY] * PEERS,...  7.76 us
    unnamed x37, local copies, waits for them, and re-layouts  4.39 us
  transfers between devices with their start and end apart: 30, of which 15 were waited for; matrix products, arithmetic and copies ran while one was open for 0% of the time, Pallas kernels for 8%

profile of v2, /device:TPU:23, one launch (start us, length us, event | category | flops | bytes accessed | tf_op | source)
XLA Modules:
  0.0 180.4 jit_solution(4719772209437415958)
XLA Ops:
  0.6 7.8 %pack_first.1 = (bf16[1416,128]{1,0:T(8,128)(2,1)}, bf16[1416,128]{1,0:T(8,128)(2,1)}, bf16[1416,128]{1,0:T(8,128)(2,1)}, bf16[1416,128]{1,0:T(8,128)(2,1)}, bf1...) custom-call(s32[1]{0:T(128)} %bitcast.me, ...), custom_call_target="tpu_custom_call" | custom-call | tf_op jit(solution)/shard_map/pack_first/pallas_call | solution.py:83
  8.4 0.0 copy-start
  8.5 2.6 %copy-done = f32[8,128,1408]{2,1,0:T(8,128)S(1)} copy-done((f32[8,128,1408]{2,1,0:T(8,128)S(1)}, f32[8,128,1408]{2,1,0:T(8,128)}, u32[]{:S(2)}) %copy-start) | copy-done | bytes 5767192
  11.1 1.0 copy-done.1
  12.2 8.3 %pack_last.1 = (bf16[704,128]{1,0:T(8,128)(2,1)S(1)}, bf16[704,128]{1,0:T(8,128)(2,1)S(1)}, bf16[704,128]{1,0:T(8,128)(2,1)S(1)}, bf16[704,128]{1,0:T(8,128)(2,1...) custom-call(s32[1]{0:T(128)} %bitcast.me, ...), custom_call_target="tpu_custom_call" | custom-call | tf_op jit(solution)/shard_map/pack_last/pallas_call | solution.py:113
  20.5 1.0 collective-permute-start.15
  21.5 1.4 collective-permute-start.16
  23.0 1.3 collective-permute-start.17
  24.3 1.1 collective-permute-start.18
  25.3 1.1 collective-permute-start.19
  26.5 0.5 collective-permute-done.15.rest_1_
  26.9 1.3 collective-permute-start.20
  28.2 1.5 collective-permute-done.16.rest_2_
  29.7 1.3 collective-permute-start.21
  31.0 1.9 %collective-permute-done.17.rest_3_ = bf16[704,128]{1,0:T(8,128)(2,1)S(1)} collective-permute-done((bf16[704,128]{1,0:T(8,128)(2,1)S(1)}, bf16[704,128]{1,0:T(8,128)(2,1)S(1)}, u32[]{:S(2)}, u32[]{:S(2)}) %collective-permute-start.17) | collective-permute-done | bytes 180256 | tf_op jit(solution)/shard_map/ppermute | solution.py:252
  32.9 1.4 collective-permute-start.22
  34.2 0.0 collective-permute-done.18.rest_4_
  34.3 0.8 collective-permute-start.23
  35.0 0.5 collective-permute-done.19.rest_5_
  35.6 2.0 %collective-permute-start.24 = (bf16[704,128]{1,0:T(8,128)(2,1)S(1)}, bf16[704,128]{1,0:T(8,128)(2,1)S(1)}, u32[]{:S(2)}, u32[]{:S(2)}) collective-permute-start(bf16[704,128]{1,0:T(8,128)(2,1)S(1)} %get-tuple-element.74), channel_id=1, source_target_pairs={{0,14},{1,15},{2,12},{3,13},{4,2},{5,3},{6,0},{7,1},{8,6},{9,7},{1... | collective-permute-start | bytes 540680 | tf_op jit(solution)/shard_map/ppermute | solution.py:252
  37.5 0.2 collective-permute-done.20.rest_6_
  37.7 1.8 %collective-permute-start = (bf16[1416,128]{1,0:T(8,128)(2,1)S(1)}, bf16[1416,128]{1,0:T(8,128)(2,1)S(1)}, u32[]{:S(2)}, u32[]{:S(2)}) collective-permute-start(bf16[1416,128]{1,0:T(8,128)(2,1)S(1)} %copy-done.17), channel_id=1, source_target_pairs={{0,5},{1,6},{2,7},{3,4},{4,9},{5,10},{6,11},{7,8},{8,13},{9,14},{1... | collective-permute-start | bytes 1087496 | tf_op jit(solution)/shard_map/ppermute | solution.py:252
  39.5 0.9 collective-permute-done.21.rest_7_
  40.4 0.3 collective-permute-start.1
  40.7 2.0 %collective-permute-done.22.rest_8_ = bf16[704,128]{1,0:T(8,128)(2,1)S(1)} collective-permute-done((bf16[704,128]{1,0:T(8,128)(2,1)S(1)}, bf16[704,128]{1,0:T(8,128)(2,1)S(1)}, u32[]{:S(2)}, u32[]{:S(2)}) %collective-permute-start.22) | collective-permute-done | bytes 180256 | tf_op jit(solution)/shard_map/ppermute | solution.py:252
  42.7 1.8 collective-permute-start.10
  44.5 0.0 collective-permute-done.23.rest_9_
  44.5 4.1 %collective-permute-start.11 = (bf16[1416,128]{1,0:T(8,128)(2,1)S(1)}, bf16[1416,128]{1,0:T(8,128)(2,1)S(1)}, u32[]{:S(2)}, u32[]{:S(2)}) collective-permute-start(bf16[1416,128]{1,0:T(8,128)(2,1)S(1)} %copy-done.14), channel_id=1, source_target_pairs={{0,9},{1,10},{2,11},{3,8},{4,13},{5,14},{6,15},{7,12},{8,1},{9,2},... | collective-permute-start | bytes 1087496 | tf_op jit(solution)/shard_map/ppermute | solution.py:252
  48.6 0.0 collective-permute-done.24.rest_10_
  48.6 0.0 collective-permute-start.12
  48.6 1.8 %collective-permute-done.rest_1_ = bf16[1416,128]{1,0:T(8,128)(2,1)S(1)} collective-permute-done((bf16[1416,128]{1,0:T(8,128)(2,1)S(1)}, bf16[1416,128]{1,0:T(8,128)(2,1)S(1)}, u32[]{:S(2)}, u32[]{:S(2)}) %collective-permute-start) | collective-permute-done | bytes 362528 | tf_op jit(solution)/shard_map/ppermute | solution.py:252
  50.4 2.0 %collective-permute-start.13 = (bf16[1416,128]{1,0:T(8,128)(2,1)S(1)}, bf16[1416,128]{1,0:T(8,128)(2,1)S(1)}, u32[]{:S(2)}, u32[]{:S(2)}) collective-permute-start(bf16[1416,128]{1,0:T(8,128)(2,1)S(1)} %copy-done.12), channel_id=1, source_target_pairs={{0,11},{1,8},{2,9},{3,10},{4,15},{5,12},{6,13},{7,14},{8,3},{9,0},... | collective-permute-start | bytes 1087496 | tf_op jit(solution)/shard_map/ppermute | solution.py:252
  52.4 0.0 collective-permute-done.1.rest_2_
  52.4 5.4 %collective-permute-start.14 = (bf16[1416,128]{1,0:T(8,128)(2,1)S(1)}, bf16[1416,128]{1,0:T(8,128)(2,1)S(1)}, u32[]{:S(2)}, u32[]{:S(2)}) collective-permute-start(bf16[1416,128]{1,0:T(8,128)(2,1)S(1)} %copy-done.11), channel_id=1, source_target_pairs={{0,1},{1,2},{2,3},{3,0},{4,5},{5,6},{6,7},{7,4},{8,9},{9,10},{10,1... | collective-permute-start | bytes 1087496 | tf_op jit(solution)/shard_map/ppermute | solution.py:252
  57.8 7.3 %collective-permute-done.10.rest_11_ = bf16[1416,128]{1,0:T(8,128)(2,1)S(1)} collective-permute-done((bf16[1416,128]{1,0:T(8,128)(2,1)S(1)}, bf16[1416,128]{1,0:T(8,128)(2,1)S(1)}, u32[]{:S(2)}, u32[]{:S(2)}) %collective-permute-start.10) | collective-permute-done | bytes 362528 | tf_op jit(solution)/shard_map/ppermute | solution.py:252
  65.1 6.2 %collective-permute-start.2 = (bf16[1416,128]{1,0:T(8,128)(2,1)S(1)}, bf16[1416,128]{1,0:T(8,128)(2,1)S(1)}, u32[]{:S(2)}, u32[]{:S(2)}) collective-permute-start(bf16[1416,128]{1,0:T(8,128)(2,1)S(1)} %copy-done.10), channel_id=1, source_target_pairs={{0,13},{1,14},{2,15},{3,12},{4,1},{5,2},{6,3},{7,0},{8,5},{9,6},{1... | collective-permute-start | bytes 1087496 | tf_op jit(solution)/shard_map/ppermute | solution.py:252
  71.3 0.0 collective-permute-done.11.rest_12_
  71.3 0.0 collective-permute-start.3
  71.3 0.0 collective-permute-done.12.rest_13_
  71.3 3.0 %collective-permute-start.4 = (bf16[1416,128]{1,0:T(8,128)(2,1)S(1)}, bf16[1416,128]{1,0:T(8,128)(2,1)S(1)}, u32[]{:S(2)}, u32[]{:S(2)}) collective-permute-start(bf16[1416,128]{1,0:T(8,128)(2,1)S(1)} %copy-done.8), channel_id=1, source_target_pairs={{0,2},{1,3},{2,0},{3,1},{4,6},{5,7},{6,4},{7,5},{8,10},{9,11},{10,... | collective-permute-start | bytes 1087496 | tf_op jit(solution)/shard_map/ppermute | solution.py:252
  74.3 0.0 collective-permute-done.13.rest_14_
  74.3 2.4 %collective-permute-start.5 = (bf16[1416,128]{1,0:T(8,128)(2,1)S(1)}, bf16[1416,128]{1,0:T(8,128)(2,1)S(1)}, u32[]{:S(2)}, u32[]{:S(2)}) collective-permute-start(bf16[1416,128]{1,0:T(8,128)(2,1)S(1)} %copy-done.7), channel_id=1, source_target_pairs={{0,8},{1,9},{2,10},{3,11},{4,12},{5,13},{6,14},{7,15},{8,0},{9,1},... | collective-permute-start | bytes 1087496 | tf_op jit(solution)/shard_map/ppermute | solution.py:252
  76.8 0.0 collective-permute-done.14.rest_15_
  76.8 0.5 collective-permute-start.6
  77.3 0.4 collective-permute-done.2.rest_3_
  77.7 8.0 %collective-permute-start.7 = (bf16[1416,128]{1,0:T(8,128)(2,1)S(1)}, bf16[1416,128]{1,0:T(8,128)(2,1)S(1)}, u32[]{:S(2)}, u32[]{:S(2)}) collective-permute-start(bf16[1416,128]{1,0:T(8,128)(2,1)S(1)} %copy-done.5), channel_id=1, source_target_pairs={{0,6},{1,7},{2,4},{3,5},{4,10},{5,11},{6,8},{7,9},{8,14},{9,15},{1... | collective-permute-start | bytes 1087496 | tf_op jit(solution)/shard_map/ppermute | solution.py:252
  85.7 0.0 collective-permute-done.3.rest_4_
  85.7 0.0 collective-permute-start.8
  85.7 3.6 %collective-permute-done.4.rest_5_ = bf16[1416,128]{1,0:T(8,128)(2,1)S(1)} collective-permute-done((bf16[1416,128]{1,0:T(8,128)(2,1)S(1)}, bf16[1416,128]{1,0:T(8,128)(2,1)S(1)}, u32[]{:S(2)}, u32[]{:S(2)}) %collective-permute-start.4) | collective-permute-done | bytes 362528 | tf_op jit(solution)/shard_map/ppermute | solution.py:252
  89.3 2.9 %collective-permute-start.9 = (bf16[1416,128]{1,0:T(8,128)(2,1)S(1)}, bf16[1416,128]{1,0:T(8,128)(2,1)S(1)}, u32[]{:S(2)}, u32[]{:S(2)}) collective-permute-start(bf16[1416,128]{1,0:T(8,128)(2,1)S(1)} %copy-done.3), channel_id=1, source_target_pairs={{0,14},{1,15},{2,12},{3,13},{4,2},{5,3},{6,0},{7,1},{8,6},{9,7},{1... | collective-permute-start | bytes 1087496 | tf_op jit(solution)/shard_map/ppermute | solution.py:252
  92.2 10.6 %collective-permute-done.5.rest_6_ = bf16[1416,128]{1,0:T(8,128)(2,1)S(1)} collective-permute-done((bf16[1416,128]{1,0:T(8,128)(2,1)S(1)}, bf16[1416,128]{1,0:T(8,128)(2,1)S(1)}, u32[]{:S(2)}, u32[]{:S(2)}) %collective-permute-start.5) | collective-permute-done | bytes 362528 | tf_op jit(solution)/shard_map/ppermute | solution.py:252
  102.9 0.0 collective-permute-start.25
  102.9 0.9 collective-permute-done.6.rest_7_
  103.8 2.1 %collective-permute-start.26 = (bf16[704,128]{1,0:T(8,128)(2,1)S(1)}, bf16[704,128]{1,0:T(8,128)(2,1)S(1)}, u32[]{:S(2)}, u32[]{:S(2)}) collective-permute-start(bf16[704,128]{1,0:T(8,128)(2,1)S(1)} %get-tuple-element.76), channel_id=1, source_target_pairs={{0,9},{1,10},{2,11},{3,8},{4,13},{5,14},{6,15},{7,12},{8,1},{9,2},... | collective-permute-start | bytes 540680 | tf_op jit(solution)/shard_map/ppermute | solution.py:252
  105.9 0.7 collective-permute-done.7.rest_8_
  106.6 1.6 collective-permute-start.27
  108.2 0.0 collective-permute-done.8.rest_9_
  108.2 6.8 %collective-permute-start.28 = (bf16[704,128]{1,0:T(8,128)(2,1)S(1)}, bf16[704,128]{1,0:T(8,128)(2,1)S(1)}, u32[]{:S(2)}, u32[]{:S(2)}) collective-permute-start(bf16[704,128]{1,0:T(8,128)(2,1)S(1)} %get-tuple-element.78), channel_id=1, source_target_pairs={{0,11},{1,8},{2,9},{3,10},{4,15},{5,12},{6,13},{7,14},{8,3},{9,0},... | collective-permute-start | bytes 540680 | tf_op jit(solution)/shard_map/ppermute | solution.py:252
  115.0 5.2 %collective-permute-done.9.rest_10_ = bf16[1416,128]{1,0:T(8,128)(2,1)S(1)} collective-permute-done((bf16[1416,128]{1,0:T(8,128)(2,1)S(1)}, bf16[1416,128]{1,0:T(8,128)(2,1)S(1)}, u32[]{:S(2)}, u32[]{:S(2)}) %collective-permute-start.9) | collective-permute-done | bytes 362528 | tf_op jit(solution)/shard_map/ppermute | solution.py:252
  120.2 14.4 %finish_first.1 = (bf16[8,88,2048]{2,1,0:T(8,128)(2,1)}, f32[8,88]{1,0:T(8,128)}, bf16[8,88,2048]{2,1,0:T(8,128)(2,1)}, f32[8,88]{1,0:T(8,128)}, bf16[8,2048]{1,0:T(8,128)(2,1)S(1)}) custom-call(s32[1]{0:T(128)} %bitcast.me, bf16[1416,128]{1,0:T(8,128)(2,1)S(1)} %copy-done.2, bf16[1416,128]{1,0:T(8,128)(2,1)S(1)} %collective-permute-done.rest_1_, ...), custom_call_target="tpu_custom_call" | custom-call | tf_op jit(solution)/shard_map/finish_first/pallas_call | solution.py:215
  134.5 37.4 %all_gather.3._ = bf16[64,2048]{1,0:T(8,128)(2,1)S(1)} all-gather(bf16[8,2048]{1,0:T(8,128)(2,1)S(1)} %get-tuple-element.63), channel_id=1, replica_groups=mesh['ep'=8,'fsdp'=16] {'ep'}, dimensions={0}, use_global_device_ids=true | all-gather | bytes 294912 | tf_op jit(solution)/shard_map/all_gather | solution.py:264
  171.9 0.0 collective-permute-done.28.rest_14_
  172.0 7.8 %finish_last.1 = (bf16[8,88,2048]{2,1,0:T(8,128)(2,1)}, f32[8,88]{1,0:T(8,128)}) custom-call(s32[1]{0:T(128)} %bitcast.me, bf16[64,2048]{1,0:T(8,128)(2,1)S(1)} %all_gather.3._, bf16[704,128]{1,0:T(8,128)(2,1)S(1)} %get-tuple-element.64.rest_0_, bf16[704,128]{1,0:T(8,128)(2,1)S(1)} %collective-permute-done.15.rest_1_, ...), custom_call_target="tpu_custom_call" | custom-call | tf_op jit(solution)/shard_map/finish_last/pallas_call | solution.py:232
  179.7 0.7 copy.13
  (38 shorter events, 0.1 us)
Async XLA Ops:
  8.4 2.6 %copy-start = (f32[8,128,1408]{2,1,0:T(8,128)S(1)}, f32[8,128,1408]{2,1,0:T(8,128)}, u32[]{:S(2)}) copy-start(f32[8,128,1408]{2,1,0:T(8,128)} %up.1) | copy-start | bytes 17301508
  11.1 1.0 copy-start.1
  12.1 25.6 %copy-start.17 = (bf16[1416,128]{1,0:T(8,128)(2,1)S(1)}, bf16[1416,128]{1,0:T(8,128)(2,1)}, u32[]{:S(2)}) copy-start(bf16[1416,128]{1,0:T(8,128)(2,1)} %get-tuple-element.47) | copy-start | bytes 1087492
  12.1 28.3 %copy-start.16 = (bf16[1416,128]{1,0:T(8,128)(2,1)S(1)}, bf16[1416,128]{1,0:T(8,128)(2,1)}, u32[]{:S(2)}) copy-start(bf16[1416,128]{1,0:T(8,128)(2,1)} %get-tuple-element.48) | copy-start | bytes 1087492
  12.1 30.6 %copy-start.15 = (bf16[1416,128]{1,0:T(8,128)(2,1)S(1)}, bf16[1416,128]{1,0:T(8,128)(2,1)}, u32[]{:S(2)}) copy-start(bf16[1416,128]{1,0:T(8,128)(2,1)} %get-tuple-element.57) | copy-start | bytes 1087492
  12.1 32.4 %copy-start.14 = (bf16[1416,128]{1,0:T(8,128)(2,1)S(1)}, bf16[1416,128]{1,0:T(8,128)(2,1)}, u32[]{:S(2)}) copy-start(bf16[1416,128]{1,0:T(8,128)(2,1)} %get-tuple-element.58) | copy-start | bytes 1087492
  12.1 36.5 %copy-start.13 = (bf16[1416,128]{1,0:T(8,128)(2,1)S(1)}, bf16[1416,128]{1,0:T(8,128)(2,1)}, u32[]{:S(2)}) copy-start(bf16[1416,128]{1,0:T(8,128)(2,1)} %get-tuple-element.59) | copy-start | bytes 1087492
  12.1 38.4 %copy-start.12 = (bf16[1416,128]{1,0:T(8,128)(2,1)S(1)}, bf16[1416,128]{1,0:T(8,128)(2,1)}, u32[]{:S(2)}) copy-start(bf16[1416,128]{1,0:T(8,128)(2,1)} %get-tuple-element.60) | copy-start | bytes 1087492
  12.1 40.3 %copy-start.11 = (bf16[1416,128]{1,0:T(8,128)(2,1)S(1)}, bf16[1416,128]{1,0:T(8,128)(2,1)}, u32[]{:S(2)}) copy-start(bf16[1416,128]{1,0:T(8,128)(2,1)} %get-tuple-element.61) | copy-start | bytes 1087492
  12.1 53.0 %copy-start.10 = (bf16[1416,128]{1,0:T(8,128)(2,1)S(1)}, bf16[1416,128]{1,0:T(8,128)(2,1)}, u32[]{:S(2)}) copy-start(bf16[1416,128]{1,0:T(8,128)(2,1)} %get-tuple-element.49) | copy-start | bytes 1087492
  12.1 59.1 %copy-start.9 = (bf16[1416,128]{1,0:T(8,128)(2,1)S(1)}, bf16[1416,128]{1,0:T(8,128)(2,1)}, u32[]{:S(2)}) copy-start(bf16[1416,128]{1,0:T(8,128)(2,1)} %get-tuple-element.50) | copy-start | bytes 1087492
  12.1 59.2 %copy-start.8 = (bf16[1416,128]{1,0:T(8,128)(2,1)S(1)}, bf16[1416,128]{1,0:T(8,128)(2,1)}, u32[]{:S(2)}) copy-start(bf16[1416,128]{1,0:T(8,128)(2,1)} %get-tuple-element.51) | copy-start | bytes 1087492
  12.1 62.2 %copy-start.7 = (bf16[1416,128]{1,0:T(8,128)(2,1)S(1)}, bf16[1416,128]{1,0:T(8,128)(2,1)}, u32[]{:S(2)}) copy-start(bf16[1416,128]{1,0:T(8,128)(2,1)} %get-tuple-element.52) | copy-start | bytes 1087492
  12.2 64.6 %copy-start.6 = (bf16[1416,128]{1,0:T(8,128)(2,1)S(1)}, bf16[1416,128]{1,0:T(8,128)(2,1)}, u32[]{:S(2)}) copy-start(bf16[1416,128]{1,0:T(8,128)(2,1)} %get-tuple-element.53) | copy-start | bytes 1087492
  12.2 65.5 %copy-start.5 = (bf16[1416,128]{1,0:T(8,128)(2,1)S(1)}, bf16[1416,128]{1,0:T(8,128)(2,1)}, u32[]{:S(2)}) copy-start(bf16[1416,128]{1,0:T(8,128)(2,1)} %get-tuple-element.54) | copy-start | bytes 1087492
  12.2 73.5 %copy-start.4 = (bf16[1416,128]{1,0:T(8,128)(2,1)S(1)}, bf16[1416,128]{1,0:T(8,128)(2,1)}, u32[]{:S(2)}) copy-start(bf16[1416,128]{1,0:T(8,128)(2,1)} %get-tuple-element.55) | copy-start | bytes 1087492
  12.2 77.1 %copy-start.3 = (bf16[1416,128]{1,0:T(8,128)(2,1)S(1)}, bf16[1416,128]{1,0:T(8,128)(2,1)}, u32[]{:S(2)}) copy-start(bf16[1416,128]{1,0:T(8,128)(2,1)} %get-tuple-element.56) | copy-start | bytes 1087492
  12.2 108.0 %copy-start.2 = (bf16[1416,128]{1,0:T(8,128)(2,1)S(1)}, bf16[1416,128]{1,0:T(8,128)(2,1)}, u32[]{:S(2)}) copy-start(bf16[1416,128]{1,0:T(8,128)(2,1)} %get-tuple-element.46.rest_0_._) | copy-start | bytes 1087492
  20.5 6.4 %collective-permute-start.15 = (bf16[704,128]{1,0:T(8,128)(2,1)S(1)}, bf16[704,128]{1,0:T(8,128)(2,1)S(1)}, u32[]{:S(2)}, u32[]{:S(2)}) collective-permute-start(bf16[704,128]{1,0:T(8,128)(2,1)S(1)} %get-tuple-element.65), channel_id=1, source_target_pairs={{0,5},{1,6},{2,7},{3,4},{4,9},{5,10},{6,11},{7,8},{8,13},{9,14},{1... | collective-permute-start | bytes 540680 | tf_op jit(solution)/shard_map/ppermute | solution.py:252
  21.5 8.2 %collective-permute-start.16 = (bf16[704,128]{1,0:T(8,128)(2,1)S(1)}, bf16[704,128]{1,0:T(8,128)(2,1)S(1)}, u32[]{:S(2)}, u32[]{:S(2)}) collective-permute-start(bf16[704,128]{1,0:T(8,128)(2,1)S(1)} %get-tuple-element.66), channel_id=1, source_target_pairs={{0,15},{1,12},{2,13},{3,14},{4,3},{5,0},{6,1},{7,2},{8,7},{9,4},{1... | collective-permute-start | bytes 540680 | tf_op jit(solution)/shard_map/ppermute | solution.py:252
  23.0 9.9 %collective-permute-start.17 = (bf16[704,128]{1,0:T(8,128)(2,1)S(1)}, bf16[704,128]{1,0:T(8,128)(2,1)S(1)}, u32[]{:S(2)}, u32[]{:S(2)}) collective-permute-start(bf16[704,128]{1,0:T(8,128)(2,1)S(1)} %get-tuple-element.67), channel_id=1, source_target_pairs={{0,13},{1,14},{2,15},{3,12},{4,1},{5,2},{6,3},{7,0},{8,5},{9,6},{1... | collective-permute-start | bytes 540680 | tf_op jit(solution)/shard_map/ppermute | solution.py:252
  24.3 10.0 %collective-permute-start.18 = (bf16[704,128]{1,0:T(8,128)(2,1)S(1)}, bf16[704,128]{1,0:T(8,128)(2,1)S(1)}, u32[]{:S(2)}, u32[]{:S(2)}) collective-permute-start(bf16[704,128]{1,0:T(8,128)(2,1)S(1)} %get-tuple-element.68), channel_id=1, source_target_pairs={{0,7},{1,4},{2,5},{3,6},{4,11},{5,8},{6,9},{7,10},{8,15},{9,12},{1... | collective-permute-start | bytes 540680 | tf_op jit(solution)/shard_map/ppermute | solution.py:252
  25.3 10.2 %collective-permute-start.19 = (bf16[704,128]{1,0:T(8,128)(2,1)S(1)}, bf16[704,128]{1,0:T(8,128)(2,1)S(1)}, u32[]{:S(2)}, u32[]{:S(2)}) collective-permute-start(bf16[704,128]{1,0:T(8,128)(2,1)S(1)} %get-tuple-element.69), channel_id=1, source_target_pairs={{0,2},{1,3},{2,0},{3,1},{4,6},{5,7},{6,4},{7,5},{8,10},{9,11},{10,... | collective-permute-start | bytes 540680 | tf_op jit(solution)/shard_map/ppermute | solution.py:252
  26.9 10.8 %collective-permute-start.20 = (bf16[704,128]{1,0:T(8,128)(2,1)S(1)}, bf16[704,128]{1,0:T(8,128)(2,1)S(1)}, u32[]{:S(2)}, u32[]{:S(2)}) collective-permute-start(bf16[704,128]{1,0:T(8,128)(2,1)S(1)} %get-tuple-element.70), channel_id=1, source_target_pairs={{0,8},{1,9},{2,10},{3,11},{4,12},{5,13},{6,14},{7,15},{8,0},{9,1},... | collective-permute-start | bytes 540680 | tf_op jit(solution)/shard_map/ppermute | solution.py:252
  29.7 10.7 %collective-permute-start.21 = (bf16[704,128]{1,0:T(8,128)(2,1)S(1)}, bf16[704,128]{1,0:T(8,128)(2,1)S(1)}, u32[]{:S(2)}, u32[]{:S(2)}) collective-permute-start(bf16[704,128]{1,0:T(8,128)(2,1)S(1)} %get-tuple-element.71), channel_id=1, source_target_pairs={{0,10},{1,11},{2,8},{3,9},{4,14},{5,15},{6,12},{7,13},{8,2},{9,3},... | collective-permute-start | bytes 540680 | tf_op jit(solution)/shard_map/ppermute | solution.py:252
  32.9 9.8 %collective-permute-start.22 = (bf16[704,128]{1,0:T(8,128)(2,1)S(1)}, bf16[704,128]{1,0:T(8,128)(2,1)S(1)}, u32[]{:S(2)}, u32[]{:S(2)}) collective-permute-start(bf16[704,128]{1,0:T(8,128)(2,1)S(1)} %get-tuple-element.72), channel_id=1, source_target_pairs={{0,6},{1,7},{2,4},{3,5},{4,10},{5,11},{6,8},{7,9},{8,14},{9,15},{1... | collective-permute-start | bytes 540680 | tf_op jit(solution)/shard_map/ppermute | solution.py:252
  34.3 10.2 %collective-permute-start.23 = (bf16[704,128]{1,0:T(8,128)(2,1)S(1)}, bf16[704,128]{1,0:T(8,128)(2,1)S(1)}, u32[]{:S(2)}, u32[]{:S(2)}) collective-permute-start(bf16[704,128]{1,0:T(8,128)(2,1)S(1)} %get-tuple-element.73), channel_id=1, source_target_pairs={{0,12},{1,13},{2,14},{3,15},{4,0},{5,1},{6,2},{7,3},{8,4},{9,5},{1... | collective-permute-start | bytes 540680 | tf_op jit(solution)/shard_map/ppermute | solution.py:252
  35.6 13.0 %collective-permute-start.24 = (bf16[704,128]{1,0:T(8,128)(2,1)S(1)}, bf16[704,128]{1,0:T(8,128)(2,1)S(1)}, u32[]{:S(2)}, u32[]{:S(2)}) collective-permute-start(bf16[704,128]{1,0:T(8,128)(2,1)S(1)} %get-tuple-element.74), channel_id=1, source_target_pairs={{0,14},{1,15},{2,12},{3,13},{4,2},{5,3},{6,0},{7,1},{8,6},{9,7},{1... | collective-permute-start | bytes 540680 | tf_op jit(solution)/shard_map/ppermute | solution.py:252
  37.7 12.7 %collective-permute-start = (bf16[1416,128]{1,0:T(8,128)(2,1)S(1)}, bf16[1416,128]{1,0:T(8,128)(2,1)S(1)}, u32[]{:S(2)}, u32[]{:S(2)}) collective-permute-start(bf16[1416,128]{1,0:T(8,128)(2,1)S(1)} %copy-done.17), channel_id=1, source_target_pairs={{0,5},{1,6},{2,7},{3,4},{4,9},{5,10},{6,11},{7,8},{8,13},{9,14},{1... | collective-permute-start | bytes 1087496 | tf_op jit(solution)/shard_map/ppermute | solution.py:252
  40.4 12.0 %collective-permute-start.1 = (bf16[1416,128]{1,0:T(8,128)(2,1)S(1)}, bf16[1416,128]{1,0:T(8,128)(2,1)S(1)}, u32[]{:S(2)}, u32[]{:S(2)}) collective-permute-start(bf16[1416,128]{1,0:T(8,128)(2,1)S(1)} %copy-done.16), channel_id=1, source_target_pairs={{0,15},{1,12},{2,13},{3,14},{4,3},{5,0},{6,1},{7,2},{8,7},{9,4},{1... | collective-permute-start | bytes 1087496 | tf_op jit(solution)/shard_map/ppermute | solution.py:252
  42.7 22.4 %collective-permute-start.10 = (bf16[1416,128]{1,0:T(8,128)(2,1)S(1)}, bf16[1416,128]{1,0:T(8,128)(2,1)S(1)}, u32[]{:S(2)}, u32[]{:S(2)}) collective-permute-start(bf16[1416,128]{1,0:T(8,128)(2,1)S(1)} %copy-done.15), channel_id=1, source_target_pairs={{0,4},{1,5},{2,6},{3,7},{4,8},{5,9},{6,10},{7,11},{8,12},{9,13},{1... | collective-permute-start | bytes 1087496 | tf_op jit(solution)/shard_map/ppermute | solution.py:252
  44.5 26.8 %collective-permute-start.11 = (bf16[1416,128]{1,0:T(8,128)(2,1)S(1)}, bf16[1416,128]{1,0:T(8,128)(2,1)S(1)}, u32[]{:S(2)}, u32[]{:S(2)}) collective-permute-start(bf16[1416,128]{1,0:T(8,128)(2,1)S(1)} %copy-done.14), channel_id=1, source_target_pairs={{0,9},{1,10},{2,11},{3,8},{4,13},{5,14},{6,15},{7,12},{8,1},{9,2},... | collective-permute-start | bytes 1087496 | tf_op jit(solution)/shard_map/ppermute | solution.py:252
  48.6 22.7 %collective-permute-start.12 = (bf16[1416,128]{1,0:T(8,128)(2,1)S(1)}, bf16[1416,128]{1,0:T(8,128)(2,1)S(1)}, u32[]{:S(2)}, u32[]{:S(2)}) collective-permute-start(bf16[1416,128]{1,0:T(8,128)(2,1)S(1)} %copy-done.13), channel_id=1, source_target_pairs={{0,3},{1,0},{2,1},{3,2},{4,7},{5,4},{6,5},{7,6},{8,11},{9,8},{10,9... | collective-permute-start | bytes 1087496 | tf_op jit(solution)/shard_map/ppermute | solution.py:252
  50.4 23.9 %collective-permute-start.13 = (bf16[1416,128]{1,0:T(8,128)(2,1)S(1)}, bf16[1416,128]{1,0:T(8,128)(2,1)S(1)}, u32[]{:S(2)}, u32[]{:S(2)}) collective-permute-start(bf16[1416,128]{1,0:T(8,128)(2,1)S(1)} %copy-done.12), channel_id=1, source_target_pairs={{0,11},{1,8},{2,9},{3,10},{4,15},{5,12},{6,13},{7,14},{8,3},{9,0},... | collective-permute-start | bytes 1087496 | tf_op jit(solution)/shard_map/ppermute | solution.py:252
  52.4 24.3 %collective-permute-start.14 = (bf16[1416,128]{1,0:T(8,128)(2,1)S(1)}, bf16[1416,128]{1,0:T(8,128)(2,1)S(1)}, u32[]{:S(2)}, u32[]{:S(2)}) collective-permute-start(bf16[1416,128]{1,0:T(8,128)(2,1)S(1)} %copy-done.11), channel_id=1, source_target_pairs={{0,1},{1,2},{2,3},{3,0},{4,5},{5,6},{6,7},{7,4},{8,9},{9,10},{10,1... | collective-permute-start | bytes 1087496 | tf_op jit(solution)/shard_map/ppermute | solution.py:252
  65.1 12.6 %collective-permute-start.2 = (bf16[1416,128]{1,0:T(8,128)(2,1)S(1)}, bf16[1416,128]{1,0:T(8,128)(2,1)S(1)}, u32[]{:S(2)}, u32[]{:S(2)}) collective-permute-start(bf16[1416,128]{1,0:T(8,128)(2,1)S(1)} %copy-done.10), channel_id=1, source_target_pairs={{0,13},{1,14},{2,15},{3,12},{4,1},{5,2},{6,3},{7,0},{8,5},{9,6},{1... | collective-permute-start | bytes 1087496 | tf_op jit(solution)/shard_map/ppermute | solution.py:252
  71.3 14.4 %collective-permute-start.3 = (bf16[1416,128]{1,0:T(8,128)(2,1)S(1)}, bf16[1416,128]{1,0:T(8,128)(2,1)S(1)}, u32[]{:S(2)}, u32[]{:S(2)}) collective-permute-start(bf16[1416,128]{1,0:T(8,128)(2,1)S(1)} %copy-done.9), channel_id=1, source_target_pairs={{0,7},{1,4},{2,5},{3,6},{4,11},{5,8},{6,9},{7,10},{8,15},{9,12},{1... | collective-permute-start | bytes 1087496 | tf_op jit(solution)/shard_map/ppermute | solution.py:252
  71.3 18.0 %collective-permute-start.4 = (bf16[1416,128]{1,0:T(8,128)(2,1)S(1)}, bf16[1416,128]{1,0:T(8,128)(2,1)S(1)}, u32[]{:S(2)}, u32[]{:S(2)}) collective-permute-start(bf16[1416,128]{1,0:T(8,128)(2,1)S(1)} %copy-done.8), channel_id=1, source_target_pairs={{0,2},{1,3},{2,0},{3,1},{4,6},{5,7},{6,4},{7,5},{8,10},{9,11},{10,... | collective-permute-start | bytes 1087496 | tf_op jit(solution)/shard_map/ppermute | solution.py:252
  74.3 28.6 %collective-permute-start.5 = (bf16[1416,128]{1,0:T(8,128)(2,1)S(1)}, bf16[1416,128]{1,0:T(8,128)(2,1)S(1)}, u32[]{:S(2)}, u32[]{:S(2)}) collective-permute-start(bf16[1416,128]{1,0:T(8,128)(2,1)S(1)} %copy-done.7), channel_id=1, source_target_pairs={{0,8},{1,9},{2,10},{3,11},{4,12},{5,13},{6,14},{7,15},{8,0},{9,1},... | collective-permute-start | bytes 1087496 | tf_op jit(solution)/shard_map/ppermute | solution.py:252
  76.8 27.1 %collective-permute-start.6 = (bf16[1416,128]{1,0:T(8,128)(2,1)S(1)}, bf16[1416,128]{1,0:T(8,128)(2,1)S(1)}, u32[]{:S(2)}, u32[]{:S(2)}) collective-permute-start(bf16[1416,128]{1,0:T(8,128)(2,1)S(1)} %copy-done.6), channel_id=1, source_target_pairs={{0,10},{1,11},{2,8},{3,9},{4,14},{5,15},{6,12},{7,13},{8,2},{9,3},... | collective-permute-start | bytes 1087496 | tf_op jit(solution)/shard_map/ppermute | solution.py:252
  77.7 28.9 %collective-permute-start.7 = (bf16[1416,128]{1,0:T(8,128)(2,1)S(1)}, bf16[1416,128]{1,0:T(8,128)(2,1)S(1)}, u32[]{:S(2)}, u32[]{:S(2)}) collective-permute-start(bf16[1416,128]{1,0:T(8,128)(2,1)S(1)} %copy-done.5), channel_id=1, source_target_pairs={{0,6},{1,7},{2,4},{3,5},{4,10},{5,11},{6,8},{7,9},{8,14},{9,15},{1... | collective-permute-start | bytes 1087496 | tf_op jit(solution)/shard_map/ppermute | solution.py:252
  85.7 22.5 %collective-permute-start.8 = (bf16[1416,128]{1,0:T(8,128)(2,1)S(1)}, bf16[1416,128]{1,0:T(8,128)(2,1)S(1)}, u32[]{:S(2)}, u32[]{:S(2)}) collective-permute-start(bf16[1416,128]{1,0:T(8,128)(2,1)S(1)} %copy-done.4), channel_id=1, source_target_pairs={{0,12},{1,13},{2,14},{3,15},{4,0},{5,1},{6,2},{7,3},{8,4},{9,5},{1... | collective-permute-start | bytes 1087496 | tf_op jit(solution)/shard_map/ppermute | solution.py:252
  89.3 30.9 %collective-permute-start.9 = (bf16[1416,128]{1,0:T(8,128)(2,1)S(1)}, bf16[1416,128]{1,0:T(8,128)(2,1)S(1)}, u32[]{:S(2)}, u32[]{:S(2)}) collective-permute-start(bf16[1416,128]{1,0:T(8,128)(2,1)S(1)} %copy-done.3), channel_id=1, source_target_pairs={{0,14},{1,15},{2,12},{3,13},{4,2},{5,3},{6,0},{7,1},{8,6},{9,7},{1... | collective-permute-start | bytes 1087496 | tf_op jit(solution)/shard_map/ppermute | solution.py:252
  102.9 69.1 %collective-permute-start.25 = (bf16[704,128]{1,0:T(8,128)(2,1)S(1)}, bf16[704,128]{1,0:T(8,128)(2,1)S(1)}, u32[]{:S(2)}, u32[]{:S(2)}) collective-permute-start(bf16[704,128]{1,0:T(8,128)(2,1)S(1)} %get-tuple-element.75), channel_id=1, source_target_pairs={{0,4},{1,5},{2,6},{3,7},{4,8},{5,9},{6,10},{7,11},{8,12},{9,13},{1... | collective-permute-start | bytes 540680 | tf_op jit(solution)/shard_map/ppermute | solution.py:252
  103.8 68.1 %collective-permute-start.26 = (bf16[704,128]{1,0:T(8,128)(2,1)S(1)}, bf16[704,128]{1,0:T(8,128)(2,1)S(1)}, u32[]{:S(2)}, u32[]{:S(2)}) collective-permute-start(bf16[704,128]{1,0:T(8,128)(2,1)S(1)} %get-tuple-element.76), channel_id=1, source_target_pairs={{0,9},{1,10},{2,11},{3,8},{4,13},{5,14},{6,15},{7,12},{8,1},{9,2},... | collective-permute-start | bytes 540680 | tf_op jit(solution)/shard_map/ppermute | solution.py:252
  106.6 65.4 %collective-permute-start.27 = (bf16[704,128]{1,0:T(8,128)(2,1)S(1)}, bf16[704,128]{1,0:T(8,128)(2,1)S(1)}, u32[]{:S(2)}, u32[]{:S(2)}) collective-permute-start(bf16[704,128]{1,0:T(8,128)(2,1)S(1)} %get-tuple-element.77), channel_id=1, source_target_pairs={{0,3},{1,0},{2,1},{3,2},{4,7},{5,4},{6,5},{7,6},{8,11},{9,8},{10,9... | collective-permute-start | bytes 540680 | tf_op jit(solution)/shard_map/ppermute | solution.py:252
  108.2 63.7 %collective-permute-start.28 = (bf16[704,128]{1,0:T(8,128)(2,1)S(1)}, bf16[704,128]{1,0:T(8,128)(2,1)S(1)}, u32[]{:S(2)}, u32[]{:S(2)}) collective-permute-start(bf16[704,128]{1,0:T(8,128)(2,1)S(1)} %get-tuple-element.78), channel_id=1, source_target_pairs={{0,11},{1,8},{2,9},{3,10},{4,15},{5,12},{6,13},{7,14},{8,3},{9,0},... | collective-permute-start | bytes 540680 | tf_op jit(solution)/shard_map/ppermute | solution.py:252
  120.2 51.8 %collective-permute-start.29 = (bf16[704,128]{1,0:T(8,128)(2,1)S(1)}, bf16[704,128]{1,0:T(8,128)(2,1)S(1)}, u32[]{:S(2)}, u32[]{:S(2)}) collective-permute-start(bf16[704,128]{1,0:T(8,128)(2,1)S(1)} %get-tuple-element.79), channel_id=1, source_target_pairs={{0,1},{1,2},{2,3},{3,0},{4,5},{5,6},{6,7},{7,4},{8,9},{9,10},{10,1... | collective-permute-start | bytes 540680 | tf_op jit(solution)/shard_map/ppermute | solution.py:252

commit v3 on v2

v3 whole, which is shorter than its diff:
```python
import jax
import jax.numpy as jnp
from jax import lax
from jax.experimental import pallas as pl
from jax.experimental.pallas import tpu as pltpu
from jax.sharding import PartitionSpec as P

D_MODEL = 2048
SIDE = 4
PEERS = 16
OWN = 8
COLS = 88
LANES = 128
ROWS = OWN * COLS
FIRST_ROWS = 2 * ROWS + OWN
FIRST_LIMIT = 46

HOPS = (
    (1, 1), (3, 3),
    (3, 1), (1, 3),
    (0, 2), (2, 0),
    (2, 2),
    (1, 2), (3, 0),
    (3, 2), (1, 0),
    (2, 1), (0, 3),
    (2, 3), (0, 1),
)
HBM = pl.BlockSpec(memory_space=pltpu.HBM)
ANY = pl.BlockSpec(memory_space=pl.ANY)
VMEM = pl.BlockSpec(memory_space=pltpu.VMEM)
SMEM = pl.BlockSpec(memory_space=pltpu.SMEM)


def moved(me, hop, sign):
    y, x = me // SIDE, me % SIDE
    return (y + SIDE + sign * hop[0]) % SIDE * SIDE + (x + SIDE + sign * hop[1]) % SIDE


def started(copies):
    for copy in copies:
        copy.start()
    return copies


def peers_of(me):
    return [moved(me, hop, 1) for hop in ((0, 0), *HOPS)]


def turned_out(raw, turned, outs, peers, rows):
    whole = raw[...].astype(jnp.bfloat16).T
    for peer in range(PEERS):
        turned[peer] = whole[COLS * peer : COLS * (peer + 1), :]
    for out, peer in zip(outs, peers):
        out[rows, :] = turned[peer]


def cut_out(whole, outs, peers, rows):
    for out, peer in zip(outs, peers):
        part = whole[pl.ds(pl.multiple_of(COLS * peer, 8), COLS), :]
        out[rows, :] = part.astype(jnp.bfloat16)


def pack_first_kernel(me, gate, down, served, *rest):
    outs, (raw_gate, raw_down, turned, sems_gate, sems_down) = rest[:PEERS], rest[PEERS:]
    gates = [pltpu.make_async_copy(gate.at[e], raw_gate.at[e], sems_gate.at[e]) for e in range(OWN)]
    downs = [pltpu.make_async_copy(down.at[e], raw_down.at[e], sems_down.at[e]) for e in range(OWN)]
    for e in range(OWN):
        gates[e].start()
        downs[e].start()
    peers = peers_of(me[0])
    for out in outs:
        out[2 * ROWS :, :] = served[...]
    for e in range(OWN):
        rows = slice(COLS * e, COLS * (e + 1))
        gates[e].wait()
        turned_out(
            raw_gate.at[e], turned.at[e % 2], outs, peers, slice(ROWS + rows.start, ROWS + rows.stop)
        )
        downs[e].wait()
        cut_out(raw_down.at[e], outs, peers, rows)


def pack_first(me, gate, down, served):
    return pl.pallas_call(
        pack_first_kernel,
        in_specs=[SMEM, HBM, HBM, VMEM],
        out_specs=[VMEM] * PEERS,
        out_shape=[jax.ShapeDtypeStruct((FIRST_ROWS, LANES), jnp.bfloat16)] * PEERS,
        scratch_shapes=[
            pltpu.VMEM((OWN, LANES, PEERS * COLS), jnp.float32),
            pltpu.VMEM((OWN, PEERS * COLS, LANES), jnp.float32),
            pltpu.VMEM((2, PEERS, COLS, LANES), jnp.bfloat16),
            pltpu.SemaphoreType.DMA((OWN,)),
            pltpu.SemaphoreType.DMA((OWN,)),
        ],
        compiler_params=pltpu.CompilerParams(vmem_limit_bytes=FIRST_LIMIT << 20),
        name="pack_first",
    )(me, gate, down, served)


def pack_last_kernel(me, up, _, *rest):
    outs, (raw, turned, sems) = rest[:PEERS], rest[PEERS:]
    copies = started([pltpu.make_async_copy(up.at[e], raw.at[e], sems.at[e]) for e in range(OWN)])
    peers = peers_of(me[0])
    for e in range(OWN):
        copies[e].wait()
        turned_out(
            raw.at[e], turned.at[e % 2], outs, peers, slice(COLS * e, COLS * (e + 1))
        )


def pack_last(me, up, after):
    return pl.pallas_call(
        pack_last_kernel,
        in_specs=[SMEM, HBM, ANY],
        out_specs=[VMEM] * PEERS,
        out_shape=[jax.ShapeDtypeStruct((ROWS, LANES), jnp.bfloat16)] * PEERS,
        scratch_shapes=[
            pltpu.VMEM((OWN, LANES, PEERS * COLS), jnp.float32),
            pltpu.VMEM((2, PEERS, COLS, LANES), jnp.bfloat16),
            pltpu.SemaphoreType.DMA((OWN,)),
        ],
        compiler_params=pltpu.CompilerParams(vmem_limit_bytes=10 << 20),
        name="pack_last",
    )(me, up, after)


def factor_of(parts, q, scales):
    rows = slice(COLS * q, COLS * (q + 1))
    total = jnp.abs(parts[0][rows, :].astype(jnp.float32))
    for part in parts[1:]:
        total = total + jnp.abs(part[rows, :].astype(jnp.float32))
    scales[q % OWN : q % OWN + 1, :] = jnp.sum(total.T, axis=0, keepdims=True) / D_MODEL
    return D_MODEL / jnp.sum(total, axis=1, keepdims=True)


def scaled(parts, lanes, made, q, factor):
    rows = slice(COLS * q, COLS * (q + 1))
    for part, here in zip(parts, lanes):
        made[q, :, here] = (part[rows, :].astype(jnp.float32) * factor).astype(jnp.bfloat16)


def finish_kernel(me, parts, outs, routed, made, sems):
    lanes = [
        pl.ds(pl.multiple_of(LANES * moved(me[0], hop, -1), LANES), LANES)
        for hop in ((0, 0), *HOPS)
    ]
    writes = []
    for q in range(len(outs) * OWN):
        ready, scales = outs[q // OWN]
        scaled(parts, lanes, made, q, factor_of(parts, q, scales))
        writes += started([pltpu.make_async_copy(made.at[q], ready.at[q % OWN], sems.at[q])])
    if routed is not None:
        for part, here in zip(parts, lanes):
            routed[:, here] = part[2 * ROWS :, :]
    for copy in writes:
        copy.wait()


def finish_first_kernel(me, *rest):
    parts, (down, scale_down, gate, scale_gate, routed, made, sems) = rest[:PEERS], rest[PEERS:]
    finish_kernel(me, parts, [(down, scale_down), (gate, scale_gate)], routed, made, sems)


def finish_last_kernel(me, _, *rest):
    parts, (up, scale_up, made, sems) = rest[:PEERS], rest[PEERS:]
    finish_kernel(me, parts, [(up, scale_up)], None, made, sems)


READY = jax.ShapeDtypeStruct((OWN, COLS, D_MODEL), jnp.bfloat16)
SCALE = jax.ShapeDtypeStruct((OWN, COLS), jnp.float32)
ROUTED = jax.ShapeDtypeStruct((OWN, D_MODEL), jnp.bfloat16)


def finish_first(me, parts):
    return pl.pallas_call(
        finish_first_kernel,
        in_specs=[SMEM] + [VMEM] * PEERS,
        out_specs=[HBM, VMEM, HBM, VMEM, VMEM],
        out_shape=[READY, SCALE, READY, SCALE, ROUTED],
        scratch_shapes=[
            pltpu.VMEM((2 * OWN, COLS, D_MODEL), jnp.bfloat16),
            pltpu.SemaphoreType.DMA((2 * OWN,)),
        ],
        compiler_params=pltpu.CompilerParams(vmem_limit_bytes=15 << 20),
        name="finish_first",
    )(me, *parts)


def finish_last(me, after, parts):
    return pl.pallas_call(
        finish_last_kernel,
        in_specs=[SMEM, ANY] + [VMEM] * PEERS,
        out_specs=[HBM, VMEM],
        out_shape=[READY, SCALE],
        scratch_shapes=[
            pltpu.VMEM((OWN, COLS, D_MODEL), jnp.bfloat16),
            pltpu.SemaphoreType.DMA((OWN,)),
        ],
        compiler_params=pltpu.CompilerParams(vmem_limit_bytes=9 << 20),
        name="finish_last",
    )(me, after, *parts)


def to_owners(parts):
    received = [parts[0]]
    for k, hop in enumerate(HOPS):
        route = [(d, moved(d, hop, 1)) for d in range(PEERS)]
        received.append(lax.ppermute(parts[k + 1], "fsdp", route))
    return received


def shards(train_gate, train_up, train_down, router_weight, router_gain):
    me = lax.axis_index("fsdp").astype(jnp.int32)[None]
    served = (jnp.swapaxes(router_weight, 0, 1) * router_gain[None, :]).astype(jnp.bfloat16)
    first = pack_first(me, train_gate, train_down, served)
    got_first = to_owners(first)
    last = pack_last(me, train_up, first[0])
    got_last = to_owners(last)
    ready_down, scale_down, ready_gate, scale_gate, routed = finish_first(me, got_first)
    serve_router = lax.all_gather(routed, "ep", axis=0, tiled=True)
    ready_up, scale_up = finish_last(me, serve_router, got_last)
    return (
        jnp.swapaxes(ready_gate, 1, 2),
        jnp.swapaxes(ready_up, 1, 2),
        ready_down,
        scale_gate,
        scale_up,
        scale_down,
        jnp.swapaxes(serve_router, 0, 1),
    )


def solution(mesh):
    in_specs = (
        P("ep", "fsdp", None),
        P("ep", "fsdp", None),
        P("ep", None, "fsdp"),
        P("fsdp", "ep"),
        P("fsdp"),
    )
    out_specs = (
        P("ep", None, "fsdp"),
        P("ep", None, "fsdp"),
        P("ep", "fsdp", None),
        P("ep", "fsdp"),
        P("ep", "fsdp"),
        P("ep", "fsdp"),
        P(),
    )
    return jax.shard_map(shards, mesh=mesh, in_specs=in_specs, out_specs=out_specs, check_vma=False)
```

time: 181 us -> 161 us (0.89)
  Pallas kernels: 38.3 us -> 17 us
  blocking collectives: 37.4 us -> 41.1 us
  local copies, waits for them, and re-layouts: 4.39 us -> 2.1 us
    pallas_call x4, Pallas kernels: 38.3 us -> 17 us  [the longest x1 4.95 us: finish_first(): pl.pallas_call(finish_first_kernel, in_specs=[SMEM] + [VMEM] * PEERS, out...]
    all_gather x1, blocking collectives: 37.4 us -> 41.1 us  [shards(): serve_router = lax.all_gather(routed, 'ep', axis=0, tiled=True)]
    unnamed x37 -> x3, local copies, waits for them, and re-layouts: 4.39 us -> 2.1 us
  transfers between devices with their start and end apart: 30 -> 30, of which waited for: 15 -> 14; matrix products, arithmetic and copies ran while one was open for 0% -> 0% of each run, Pallas kernels for 8% -> 3%
where the time goes in v3:
time: 161 us
  starting transfers between devices  62.2 us (39%)
  blocking collectives  41.1 us (26%)
  waiting for transfers between devices  37 us (23%)
  Pallas kernels  17 us (11%)
  local copies, waits for them, and re-layouts  2.1 us (1%)
    ppermute x30, starting transfers between devices, to_owners(): received.append(lax.ppermute(parts[k + 1], 'fsdp', route))  62.2 us
    all_gather x1, blocking collectives, shards(): serve_router = lax.all_gather(routed, 'ep', axis=0, tiled=True)  41.1 us
    ppermute x30, waiting for transfers between devices, to_owners(): received.append(lax.ppermute(parts[k + 1], 'fsdp', route))  37 us
    pallas_call x1, Pallas kernels, finish_first(): pl.pallas_call(finish_first_kernel, in_specs=[SMEM] + [VMEM] * PEERS, out...  4.95 us
    pallas_call x1, Pallas kernels, pack_first(): pl.pallas_call(pack_first_kernel, in_specs=[SMEM, HBM, HBM, VMEM], out_sp...  4.6 us
    pallas_call x1, Pallas kernels, pack_last(): pl.pallas_call(pack_last_kernel, in_specs=[SMEM, HBM, ANY], out_specs=[VM...  4.29 us
  transfers between devices with their start and end apart: 30, of which 14 were waited for; matrix products, arithmetic and copies ran while one was open for 0% of the time, Pallas kernels for 3%

profile of v3, /device:TPU:23, one launch (start us, length us, event | category | flops | bytes accessed | tf_op | source)
XLA Modules:
  0.0 160.7 jit_solution(4365929571565768791)
XLA Ops:
  0.6 0.7 fusion.served
  1.3 4.6 %pack_first.1 = (bf16[1416,128]{1,0:T(8,128)(2,1)S(1)}, bf16[1416,128]{1,0:T(8,128)(2,1)S(1)}, bf16[1416,128]{1,0:T(8,128)(2,1)S(1)}, bf16[1416,128]{1,0:T(8,128...) custom-call(s32[1]{0:T(128)} %bitcast.me, ...), custom_call_target="tpu_custom_call" | custom-call | tf_op jit(solution)/shard_map/pack_first/pallas_call | solution.py:84
  5.9 1.4 copy-done
  7.3 4.3 %pack_last.1 = (bf16[704,128]{1,0:T(8,128)(2,1)S(1)}, bf16[704,128]{1,0:T(8,128)(2,1)S(1)}, bf16[704,128]{1,0:T(8,128)(2,1)S(1)}, bf16[704,128]{1,0:T(8,128)(2,1...) custom-call(s32[1]{0:T(128)} %bitcast.me, ...), custom_call_target="tpu_custom_call" | custom-call | tf_op jit(solution)/shard_map/pack_last/pallas_call | solution.py:113
  11.6 1.0 collective-permute-start.15
  12.6 1.4 collective-permute-start.16
  14.1 1.3 collective-permute-start.17
  15.4 1.1 collective-permute-start.18
  16.4 1.1 collective-permute-start.19
  17.6 0.5 collective-permute-done.15.rest_1_
  18.0 1.3 collective-permute-start.20
  19.3 1.5 collective-permute-done.16.rest_2_
  20.8 1.3 collective-permute-start.21
  22.1 1.9 %collective-permute-done.17.rest_3_ = bf16[704,128]{1,0:T(8,128)(2,1)S(1)} collective-permute-done((bf16[704,128]{1,0:T(8,128)(2,1)S(1)}, bf16[704,128]{1,0:T(8,128)(2,1)S(1)}, u32[]{:S(2)}, u32[]{:S(2)}) %collective-permute-start.17) | collective-permute-done | bytes 180256 | tf_op jit(solution)/shard_map/ppermute | solution.py:209
  24.0 1.4 collective-permute-start.22
  25.3 0.0 collective-permute-done.18.rest_4_
  25.3 0.8 collective-permute-start.23
  26.1 0.5 collective-permute-done.19.rest_5_
  26.6 2.0 %collective-permute-start.24 = (bf16[704,128]{1,0:T(8,128)(2,1)S(1)}, bf16[704,128]{1,0:T(8,128)(2,1)S(1)}, u32[]{:S(2)}, u32[]{:S(2)}) collective-permute-start(bf16[704,128]{1,0:T(8,128)(2,1)S(1)} %get-tuple-element.74), channel_id=1, source_target_pairs={{0,14},{1,15},{2,12},{3,13},{4,2},{5,3},{6,0},{7,1},{8,6},{9,7},{1... | collective-permute-start | bytes 540680 | tf_op jit(solution)/shard_map/ppermute | solution.py:209
  28.7 0.0 collective-permute-done.20.rest_6_
  28.7 1.9 %collective-permute-start = (bf16[1416,128]{1,0:T(8,128)(2,1)S(1)}, bf16[1416,128]{1,0:T(8,128)(2,1)S(1)}, u32[]{:S(2)}, u32[]{:S(2)}) collective-permute-start(bf16[1416,128]{1,0:T(8,128)(2,1)S(1)} %get-tuple-element.47), channel_id=1, source_target_pairs={{0,5},{1,6},{2,7},{3,4},{4,9},{5,10},{6,11},{7,8},{8,13},{9,14},{1... | collective-permute-start | bytes 1087496 | tf_op jit(solution)/shard_map/ppermute | solution.py:209
  30.6 0.9 collective-permute-done.21.rest_7_
  31.5 0.3 collective-permute-start.1
  31.8 2.0 %collective-permute-done.22.rest_8_ = bf16[704,128]{1,0:T(8,128)(2,1)S(1)} collective-permute-done((bf16[704,128]{1,0:T(8,128)(2,1)S(1)}, bf16[704,128]{1,0:T(8,128)(2,1)S(1)}, u32[]{:S(2)}, u32[]{:S(2)}) %collective-permute-start.22) | collective-permute-done | bytes 180256 | tf_op jit(solution)/shard_map/ppermute | solution.py:209
  33.7 1.8 %collective-permute-start.10 = (bf16[1416,128]{1,0:T(8,128)(2,1)S(1)}, bf16[1416,128]{1,0:T(8,128)(2,1)S(1)}, u32[]{:S(2)}, u32[]{:S(2)}) collective-permute-start(bf16[1416,128]{1,0:T(8,128)(2,1)S(1)} %get-tuple-element.57), channel_id=1, source_target_pairs={{0,4},{1,5},{2,6},{3,7},{4,8},{5,9},{6,10},{7,11},{8,12},{9,13},{1... | collective-permute-start | bytes 1087496 | tf_op jit(solution)/shard_map/ppermute | solution.py:209
  35.6 0.0 collective-permute-done.23.rest_9_
  35.6 4.0 %collective-permute-start.11 = (bf16[1416,128]{1,0:T(8,128)(2,1)S(1)}, bf16[1416,128]{1,0:T(8,128)(2,1)S(1)}, u32[]{:S(2)}, u32[]{:S(2)}) collective-permute-start(bf16[1416,128]{1,0:T(8,128)(2,1)S(1)} %get-tuple-element.58), channel_id=1, source_target_pairs={{0,9},{1,10},{2,11},{3,8},{4,13},{5,14},{6,15},{7,12},{8,1},{9,2},... | collective-permute-start | bytes 1087496 | tf_op jit(solution)/shard_map/ppermute | solution.py:209
  39.6 0.0 collective-permute-done.24.rest_10_
  39.6 0.0 collective-permute-start.12
  39.6 1.9 %collective-permute-done.rest_1_ = bf16[1416,128]{1,0:T(8,128)(2,1)S(1)} collective-permute-done((bf16[1416,128]{1,0:T(8,128)(2,1)S(1)}, bf16[1416,128]{1,0:T(8,128)(2,1)S(1)}, u32[]{:S(2)}, u32[]{:S(2)}) %collective-permute-start) | collective-permute-done | bytes 362528 | tf_op jit(solution)/shard_map/ppermute | solution.py:209
  41.5 2.0 %collective-permute-start.13 = (bf16[1416,128]{1,0:T(8,128)(2,1)S(1)}, bf16[1416,128]{1,0:T(8,128)(2,1)S(1)}, u32[]{:S(2)}, u32[]{:S(2)}) collective-permute-start(bf16[1416,128]{1,0:T(8,128)(2,1)S(1)} %get-tuple-element.60), channel_id=1, source_target_pairs={{0,11},{1,8},{2,9},{3,10},{4,15},{5,12},{6,13},{7,14},{8,3},{9,0},... | collective-permute-start | bytes 1087496 | tf_op jit(solution)/shard_map/ppermute | solution.py:209
  43.6 0.0 collective-permute-done.1.rest_2_
  43.6 5.4 %collective-permute-start.14 = (bf16[1416,128]{1,0:T(8,128)(2,1)S(1)}, bf16[1416,128]{1,0:T(8,128)(2,1)S(1)}, u32[]{:S(2)}, u32[]{:S(2)}) collective-permute-start(bf16[1416,128]{1,0:T(8,128)(2,1)S(1)} %get-tuple-element.61), channel_id=1, source_target_pairs={{0,1},{1,2},{2,3},{3,0},{4,5},{5,6},{6,7},{7,4},{8,9},{9,10},{10,1... | collective-permute-start | bytes 1087496 | tf_op jit(solution)/shard_map/ppermute | solution.py:209
  48.9 7.2 %collective-permute-done.10.rest_11_ = bf16[1416,128]{1,0:T(8,128)(2,1)S(1)} collective-permute-done((bf16[1416,128]{1,0:T(8,128)(2,1)S(1)}, bf16[1416,128]{1,0:T(8,128)(2,1)S(1)}, u32[]{:S(2)}, u32[]{:S(2)}) %collective-permute-start.10) | collective-permute-done | bytes 362528 | tf_op jit(solution)/shard_map/ppermute | solution.py:209
  56.1 6.2 %collective-permute-start.2 = (bf16[1416,128]{1,0:T(8,128)(2,1)S(1)}, bf16[1416,128]{1,0:T(8,128)(2,1)S(1)}, u32[]{:S(2)}, u32[]{:S(2)}) collective-permute-start(bf16[1416,128]{1,0:T(8,128)(2,1)S(1)} %get-tuple-element.49), channel_id=1, source_target_pairs={{0,13},{1,14},{2,15},{3,12},{4,1},{5,2},{6,3},{7,0},{8,5},{9,6},{1... | collective-permute-start | bytes 1087496 | tf_op jit(solution)/shard_map/ppermute | solution.py:209
  62.3 0.0 collective-permute-done.11.rest_12_
  62.4 0.0 collective-permute-start.3
  62.4 0.0 collective-permute-done.12.rest_13_
  62.4 3.0 %collective-permute-start.4 = (bf16[1416,128]{1,0:T(8,128)(2,1)S(1)}, bf16[1416,128]{1,0:T(8,128)(2,1)S(1)}, u32[]{:S(2)}, u32[]{:S(2)}) collective-permute-start(bf16[1416,128]{1,0:T(8,128)(2,1)S(1)} %get-tuple-element.51), channel_id=1, source_target_pairs={{0,2},{1,3},{2,0},{3,1},{4,6},{5,7},{6,4},{7,5},{8,10},{9,11},{10,... | collective-permute-start | bytes 1087496 | tf_op jit(solution)/shard_map/ppermute | solution.py:209
  65.3 0.0 collective-permute-done.13.rest_14_
  65.3 2.6 %collective-permute-start.5 = (bf16[1416,128]{1,0:T(8,128)(2,1)S(1)}, bf16[1416,128]{1,0:T(8,128)(2,1)S(1)}, u32[]{:S(2)}, u32[]{:S(2)}) collective-permute-start(bf16[1416,128]{1,0:T(8,128)(2,1)S(1)} %get-tuple-element.52), channel_id=1, source_target_pairs={{0,8},{1,9},{2,10},{3,11},{4,12},{5,13},{6,14},{7,15},{8,0},{9,1},... | collective-permute-start | bytes 1087496 | tf_op jit(solution)/shard_map/ppermute | solution.py:209
  67.9 0.0 collective-permute-done.14.rest_15_
  67.9 0.5 collective-permute-start.6
  68.4 0.5 collective-permute-done.2.rest_3_
  69.0 8.5 %collective-permute-start.7 = (bf16[1416,128]{1,0:T(8,128)(2,1)S(1)}, bf16[1416,128]{1,0:T(8,128)(2,1)S(1)}, u32[]{:S(2)}, u32[]{:S(2)}) collective-permute-start(bf16[1416,128]{1,0:T(8,128)(2,1)S(1)} %get-tuple-element.54), channel_id=1, source_target_pairs={{0,6},{1,7},{2,4},{3,5},{4,10},{5,11},{6,8},{7,9},{8,14},{9,15},{1... | collective-permute-start | bytes 1087496 | tf_op jit(solution)/shard_map/ppermute | solution.py:209
  77.5 0.0 collective-permute-done.3.rest_4_
  77.5 0.0 collective-permute-start.8
  77.5 3.0 %collective-permute-done.4.rest_5_ = bf16[1416,128]{1,0:T(8,128)(2,1)S(1)} collective-permute-done((bf16[1416,128]{1,0:T(8,128)(2,1)S(1)}, bf16[1416,128]{1,0:T(8,128)(2,1)S(1)}, u32[]{:S(2)}, u32[]{:S(2)}) %collective-permute-start.4) | collective-permute-done | bytes 362528 | tf_op jit(solution)/shard_map/ppermute | solution.py:209
  80.5 2.9 %collective-permute-start.9 = (bf16[1416,128]{1,0:T(8,128)(2,1)S(1)}, bf16[1416,128]{1,0:T(8,128)(2,1)S(1)}, u32[]{:S(2)}, u32[]{:S(2)}) collective-permute-start(bf16[1416,128]{1,0:T(8,128)(2,1)S(1)} %get-tuple-element.56), channel_id=1, source_target_pairs={{0,14},{1,15},{2,12},{3,13},{4,2},{5,3},{6,0},{7,1},{8,6},{9,7},{1... | collective-permute-start | bytes 1087496 | tf_op jit(solution)/shard_map/ppermute | solution.py:209
  83.4 10.4 %collective-permute-done.5.rest_6_ = bf16[1416,128]{1,0:T(8,128)(2,1)S(1)} collective-permute-done((bf16[1416,128]{1,0:T(8,128)(2,1)S(1)}, bf16[1416,128]{1,0:T(8,128)(2,1)S(1)}, u32[]{:S(2)}, u32[]{:S(2)}) %collective-permute-start.5) | collective-permute-done | bytes 362528 | tf_op jit(solution)/shard_map/ppermute | solution.py:209
  93.8 0.0 collective-permute-start.25
  93.8 1.2 collective-permute-done.6.rest_7_
  95.0 2.0 %collective-permute-start.26 = (bf16[704,128]{1,0:T(8,128)(2,1)S(1)}, bf16[704,128]{1,0:T(8,128)(2,1)S(1)}, u32[]{:S(2)}, u32[]{:S(2)}) collective-permute-start(bf16[704,128]{1,0:T(8,128)(2,1)S(1)} %get-tuple-element.76), channel_id=1, source_target_pairs={{0,9},{1,10},{2,11},{3,8},{4,13},{5,14},{6,15},{7,12},{8,1},{9,2},... | collective-permute-start | bytes 540680 | tf_op jit(solution)/shard_map/ppermute | solution.py:209
  97.0 0.8 collective-permute-done.7.rest_8_
  97.8 1.3 collective-permute-start.27
  99.1 0.0 collective-permute-done.8.rest_9_
  99.1 7.2 %collective-permute-start.28 = (bf16[704,128]{1,0:T(8,128)(2,1)S(1)}, bf16[704,128]{1,0:T(8,128)(2,1)S(1)}, u32[]{:S(2)}, u32[]{:S(2)}) collective-permute-start(bf16[704,128]{1,0:T(8,128)(2,1)S(1)} %get-tuple-element.78), channel_id=1, source_target_pairs={{0,11},{1,8},{2,9},{3,10},{4,15},{5,12},{6,13},{7,14},{8,3},{9,0},... | collective-permute-start | bytes 540680 | tf_op jit(solution)/shard_map/ppermute | solution.py:209
  106.2 4.6 %collective-permute-done.9.rest_10_ = bf16[1416,128]{1,0:T(8,128)(2,1)S(1)} collective-permute-done((bf16[1416,128]{1,0:T(8,128)(2,1)S(1)}, bf16[1416,128]{1,0:T(8,128)(2,1)S(1)}, u32[]{:S(2)}, u32[]{:S(2)}) %collective-permute-start.9) | collective-permute-done | bytes 362528 | tf_op jit(solution)/shard_map/ppermute | solution.py:209
  110.8 0.0 collective-permute-start.29
  110.8 4.9 %finish_first.1 = (bf16[8,88,2048]{2,1,0:T(8,128)(2,1)}, f32[8,88]{1,0:T(8,128)}, bf16[8,88,2048]{2,1,0:T(8,128)(2,1)}, f32[8,88]{1,0:T(8,128)}, bf16[8,2048]{1,0:T(8,128)(2,1)S(1)}) custom-call(s32[1]{0:T(128)} %bitcast.me, bf16[1416,128]{1,0:T(8,128)(2,1)S(1)} %get-tuple-element.46.rest_0_._, bf16[1416,128]{1,0:T(8,128)(2,1)S(1)} %collective-permute-done.rest_1_, ...), custom_call_target="tpu_custom_call" | custom-call | tf_op jit(solution)/shard_map/finish_first/pallas_call | solution.py:176
  115.8 41.1 %all_gather.3._ = bf16[64,2048]{1,0:T(8,128)(2,1)S(1)} all-gather(bf16[8,2048]{1,0:T(8,128)(2,1)S(1)} %get-tuple-element.63), channel_id=1, replica_groups=mesh['ep'=8,'fsdp'=16] {'ep'}, dimensions={0}, use_global_device_ids=true | all-gather | bytes 294912 | tf_op jit(solution)/shard_map/all_gather | solution.py:221
  156.8 0.0 collective-permute-done.28.rest_14_
  156.9 3.2 %finish_last.1 = (bf16[8,88,2048]{2,1,0:T(8,128)(2,1)}, f32[8,88]{1,0:T(8,128)}) custom-call(s32[1]{0:T(128)} %bitcast.me, bf16[64,2048]{1,0:T(8,128)(2,1)S(1)} %all_gather.3._, bf16[704,128]{1,0:T(8,128)(2,1)S(1)} %get-tuple-element.64.rest_0_, bf16[704,128]{1,0:T(8,128)(2,1)S(1)} %collective-permute-done.15.rest_1_, ...), custom_call_target="tpu_custom_call" | custom-call | tf_op jit(solution)/shard_map/finish_last/pallas_call | solution.py:191
  160.0 0.7 copy.13
  (5 shorter events, 0.0 us)
Async XLA Ops:
  1.3 6.0 %copy-start = (f32[8,128,1408]{2,1,0:T(8,128)S(1)}, f32[8,128,1408]{2,1,0:T(8,128)}, u32[]{:S(2)}) copy-start(f32[8,128,1408]{2,1,0:T(8,128)} %up.1) | copy-start | bytes 17301508
  11.6 6.4 %collective-permute-start.15 = (bf16[704,128]{1,0:T(8,128)(2,1)S(1)}, bf16[704,128]{1,0:T(8,128)(2,1)S(1)}, u32[]{:S(2)}, u32[]{:S(2)}) collective-permute-start(bf16[704,128]{1,0:T(8,128)(2,1)S(1)} %get-tuple-element.65), channel_id=1, source_target_pairs={{0,5},{1,6},{2,7},{3,4},{4,9},{5,10},{6,11},{7,8},{8,13},{9,14},{1... | collective-permute-start | bytes 540680 | tf_op jit(solution)/shard_map/ppermute | solution.py:209
  12.6 8.2 %collective-permute-start.16 = (bf16[704,128]{1,0:T(8,128)(2,1)S(1)}, bf16[704,128]{1,0:T(8,128)(2,1)S(1)}, u32[]{:S(2)}, u32[]{:S(2)}) collective-permute-start(bf16[704,128]{1,0:T(8,128)(2,1)S(1)} %get-tuple-element.66), channel_id=1, source_target_pairs={{0,15},{1,12},{2,13},{3,14},{4,3},{5,0},{6,1},{7,2},{8,7},{9,4},{1... | collective-permute-start | bytes 540680 | tf_op jit(solution)/shard_map/ppermute | solution.py:209
  14.1 9.9 %collective-permute-start.17 = (bf16[704,128]{1,0:T(8,128)(2,1)S(1)}, bf16[704,128]{1,0:T(8,128)(2,1)S(1)}, u32[]{:S(2)}, u32[]{:S(2)}) collective-permute-start(bf16[704,128]{1,0:T(8,128)(2,1)S(1)} %get-tuple-element.67), channel_id=1, source_target_pairs={{0,13},{1,14},{2,15},{3,12},{4,1},{5,2},{6,3},{7,0},{8,5},{9,6},{1... | collective-permute-start | bytes 540680 | tf_op jit(solution)/shard_map/ppermute | solution.py:209
  15.4 10.0 %collective-permute-start.18 = (bf16[704,128]{1,0:T(8,128)(2,1)S(1)}, bf16[704,128]{1,0:T(8,128)(2,1)S(1)}, u32[]{:S(2)}, u32[]{:S(2)}) collective-permute-start(bf16[704,128]{1,0:T(8,128)(2,1)S(1)} %get-tuple-element.68), channel_id=1, source_target_pairs={{0,7},{1,4},{2,5},{3,6},{4,11},{5,8},{6,9},{7,10},{8,15},{9,12},{1... | collective-permute-start | bytes 540680 | tf_op jit(solution)/shard_map/ppermute | solution.py:209
  16.4 10.2 %collective-permute-start.19 = (bf16[704,128]{1,0:T(8,128)(2,1)S(1)}, bf16[704,128]{1,0:T(8,128)(2,1)S(1)}, u32[]{:S(2)}, u32[]{:S(2)}) collective-permute-start(bf16[704,128]{1,0:T(8,128)(2,1)S(1)} %get-tuple-element.69), channel_id=1, source_target_pairs={{0,2},{1,3},{2,0},{3,1},{4,6},{5,7},{6,4},{7,5},{8,10},{9,11},{10,... | collective-permute-start | bytes 540680 | tf_op jit(solution)/shard_map/ppermute | solution.py:209
  18.0 10.6 %collective-permute-start.20 = (bf16[704,128]{1,0:T(8,128)(2,1)S(1)}, bf16[704,128]{1,0:T(8,128)(2,1)S(1)}, u32[]{:S(2)}, u32[]{:S(2)}) collective-permute-start(bf16[704,128]{1,0:T(8,128)(2,1)S(1)} %get-tuple-element.70), channel_id=1, source_target_pairs={{0,8},{1,9},{2,10},{3,11},{4,12},{5,13},{6,14},{7,15},{8,0},{9,1},... | collective-permute-start | bytes 540680 | tf_op jit(solution)/shard_map/ppermute | solution.py:209
  20.8 10.7 %collective-permute-start.21 = (bf16[704,128]{1,0:T(8,128)(2,1)S(1)}, bf16[704,128]{1,0:T(8,128)(2,1)S(1)}, u32[]{:S(2)}, u32[]{:S(2)}) collective-permute-start(bf16[704,128]{1,0:T(8,128)(2,1)S(1)} %get-tuple-element.71), channel_id=1, source_target_pairs={{0,10},{1,11},{2,8},{3,9},{4,14},{5,15},{6,12},{7,13},{8,2},{9,3},... | collective-permute-start | bytes 540680 | tf_op jit(solution)/shard_map/ppermute | solution.py:209
  24.0 9.7 %collective-permute-start.22 = (bf16[704,128]{1,0:T(8,128)(2,1)S(1)}, bf16[704,128]{1,0:T(8,128)(2,1)S(1)}, u32[]{:S(2)}, u32[]{:S(2)}) collective-permute-start(bf16[704,128]{1,0:T(8,128)(2,1)S(1)} %get-tuple-element.72), channel_id=1, source_target_pairs={{0,6},{1,7},{2,4},{3,5},{4,10},{5,11},{6,8},{7,9},{8,14},{9,15},{1... | collective-permute-start | bytes 540680 | tf_op jit(solution)/shard_map/ppermute | solution.py:209
  25.3 10.2 %collective-permute-start.23 = (bf16[704,128]{1,0:T(8,128)(2,1)S(1)}, bf16[704,128]{1,0:T(8,128)(2,1)S(1)}, u32[]{:S(2)}, u32[]{:S(2)}) collective-permute-start(bf16[704,128]{1,0:T(8,128)(2,1)S(1)} %get-tuple-element.73), channel_id=1, source_target_pairs={{0,12},{1,13},{2,14},{3,15},{4,0},{5,1},{6,2},{7,3},{8,4},{9,5},{1... | collective-permute-start | bytes 540680 | tf_op jit(solution)/shard_map/ppermute | solution.py:209
  26.6 13.0 %collective-permute-start.24 = (bf16[704,128]{1,0:T(8,128)(2,1)S(1)}, bf16[704,128]{1,0:T(8,128)(2,1)S(1)}, u32[]{:S(2)}, u32[]{:S(2)}) collective-permute-start(bf16[704,128]{1,0:T(8,128)(2,1)S(1)} %get-tuple-element.74), channel_id=1, source_target_pairs={{0,14},{1,15},{2,12},{3,13},{4,2},{5,3},{6,0},{7,1},{8,6},{9,7},{1... | collective-permute-start | bytes 540680 | tf_op jit(solution)/shard_map/ppermute | solution.py:209
  28.7 12.9 %collective-permute-start = (bf16[1416,128]{1,0:T(8,128)(2,1)S(1)}, bf16[1416,128]{1,0:T(8,128)(2,1)S(1)}, u32[]{:S(2)}, u32[]{:S(2)}) collective-permute-start(bf16[1416,128]{1,0:T(8,128)(2,1)S(1)} %get-tuple-element.47), channel_id=1, source_target_pairs={{0,5},{1,6},{2,7},{3,4},{4,9},{5,10},{6,11},{7,8},{8,13},{9,14},{1... | collective-permute-start | bytes 1087496 | tf_op jit(solution)/shard_map/ppermute | solution.py:209
  31.5 12.1 %collective-permute-start.1 = (bf16[1416,128]{1,0:T(8,128)(2,1)S(1)}, bf16[1416,128]{1,0:T(8,128)(2,1)S(1)}, u32[]{:S(2)}, u32[]{:S(2)}) collective-permute-start(bf16[1416,128]{1,0:T(8,128)(2,1)S(1)} %get-tuple-element.48), channel_id=1, source_target_pairs={{0,15},{1,12},{2,13},{3,14},{4,3},{5,0},{6,1},{7,2},{8,7},{9,4},{1... | collective-permute-start | bytes 1087496 | tf_op jit(solution)/shard_map/ppermute | solution.py:209
  33.7 22.4 %collective-permute-start.10 = (bf16[1416,128]{1,0:T(8,128)(2,1)S(1)}, bf16[1416,128]{1,0:T(8,128)(2,1)S(1)}, u32[]{:S(2)}, u32[]{:S(2)}) collective-permute-start(bf16[1416,128]{1,0:T(8,128)(2,1)S(1)} %get-tuple-element.57), channel_id=1, source_target_pairs={{0,4},{1,5},{2,6},{3,7},{4,8},{5,9},{6,10},{7,11},{8,12},{9,13},{1... | collective-permute-start | bytes 1087496 | tf_op jit(solution)/shard_map/ppermute | solution.py:209
  35.6 26.8 %collective-permute-start.11 = (bf16[1416,128]{1,0:T(8,128)(2,1)S(1)}, bf16[1416,128]{1,0:T(8,128)(2,1)S(1)}, u32[]{:S(2)}, u32[]{:S(2)}) collective-permute-start(bf16[1416,128]{1,0:T(8,128)(2,1)S(1)} %get-tuple-element.58), channel_id=1, source_target_pairs={{0,9},{1,10},{2,11},{3,8},{4,13},{5,14},{6,15},{7,12},{8,1},{9,2},... | collective-permute-start | bytes 1087496 | tf_op jit(solution)/shard_map/ppermute | solution.py:209
  39.6 22.7 %collective-permute-start.12 = (bf16[1416,128]{1,0:T(8,128)(2,1)S(1)}, bf16[1416,128]{1,0:T(8,128)(2,1)S(1)}, u32[]{:S(2)}, u32[]{:S(2)}) collective-permute-start(bf16[1416,128]{1,0:T(8,128)(2,1)S(1)} %get-tuple-element.59), channel_id=1, source_target_pairs={{0,3},{1,0},{2,1},{3,2},{4,7},{5,4},{6,5},{7,6},{8,11},{9,8},{10,9... | collective-permute-start | bytes 1087496 | tf_op jit(solution)/shard_map/ppermute | solution.py:209
  41.5 23.8 %collective-permute-start.13 = (bf16[1416,128]{1,0:T(8,128)(2,1)S(1)}, bf16[1416,128]{1,0:T(8,128)(2,1)S(1)}, u32[]{:S(2)}, u32[]{:S(2)}) collective-permute-start(bf16[1416,128]{1,0:T(8,128)(2,1)S(1)} %get-tuple-element.60), channel_id=1, source_target_pairs={{0,11},{1,8},{2,9},{3,10},{4,15},{5,12},{6,13},{7,14},{8,3},{9,0},... | collective-permute-start | bytes 1087496 | tf_op jit(solution)/shard_map/ppermute | solution.py:209
  43.6 24.4 %collective-permute-start.14 = (bf16[1416,128]{1,0:T(8,128)(2,1)S(1)}, bf16[1416,128]{1,0:T(8,128)(2,1)S(1)}, u32[]{:S(2)}, u32[]{:S(2)}) collective-permute-start(bf16[1416,128]{1,0:T(8,128)(2,1)S(1)} %get-tuple-element.61), channel_id=1, source_target_pairs={{0,1},{1,2},{2,3},{3,0},{4,5},{5,6},{6,7},{7,4},{8,9},{9,10},{10,1... | collective-permute-start | bytes 1087496 | tf_op jit(solution)/shard_map/ppermute | solution.py:209
  56.1 12.8 %collective-permute-start.2 = (bf16[1416,128]{1,0:T(8,128)(2,1)S(1)}, bf16[1416,128]{1,0:T(8,128)(2,1)S(1)}, u32[]{:S(2)}, u32[]{:S(2)}) collective-permute-start(bf16[1416,128]{1,0:T(8,128)(2,1)S(1)} %get-tuple-element.49), channel_id=1, source_target_pairs={{0,13},{1,14},{2,15},{3,12},{4,1},{5,2},{6,3},{7,0},{8,5},{9,6},{1... | collective-permute-start | bytes 1087496 | tf_op jit(solution)/shard_map/ppermute | solution.py:209
  62.4 15.2 %collective-permute-start.3 = (bf16[1416,128]{1,0:T(8,128)(2,1)S(1)}, bf16[1416,128]{1,0:T(8,128)(2,1)S(1)}, u32[]{:S(2)}, u32[]{:S(2)}) collective-permute-start(bf16[1416,128]{1,0:T(8,128)(2,1)S(1)} %get-tuple-element.50), channel_id=1, source_target_pairs={{0,7},{1,4},{2,5},{3,6},{4,11},{5,8},{6,9},{7,10},{8,15},{9,12},{1... | collective-permute-start | bytes 1087496 | tf_op jit(solution)/shard_map/ppermute | solution.py:209
  62.4 18.1 %collective-permute-start.4 = (bf16[1416,128]{1,0:T(8,128)(2,1)S(1)}, bf16[1416,128]{1,0:T(8,128)(2,1)S(1)}, u32[]{:S(2)}, u32[]{:S(2)}) collective-permute-start(bf16[1416,128]{1,0:T(8,128)(2,1)S(1)} %get-tuple-element.51), channel_id=1, source_target_pairs={{0,2},{1,3},{2,0},{3,1},{4,6},{5,7},{6,4},{7,5},{8,10},{9,11},{10,... | collective-permute-start | bytes 1087496 | tf_op jit(solution)/shard_map/ppermute | solution.py:209
  65.3 28.5 %collective-permute-start.5 = (bf16[1416,128]{1,0:T(8,128)(2,1)S(1)}, bf16[1416,128]{1,0:T(8,128)(2,1)S(1)}, u32[]{:S(2)}, u32[]{:S(2)}) collective-permute-start(bf16[1416,128]{1,0:T(8,128)(2,1)S(1)} %get-tuple-element.52), channel_id=1, source_target_pairs={{0,8},{1,9},{2,10},{3,11},{4,12},{5,13},{6,14},{7,15},{8,0},{9,1},... | collective-permute-start | bytes 1087496 | tf_op jit(solution)/shard_map/ppermute | solution.py:209
  67.9 27.1 %collective-permute-start.6 = (bf16[1416,128]{1,0:T(8,128)(2,1)S(1)}, bf16[1416,128]{1,0:T(8,128)(2,1)S(1)}, u32[]{:S(2)}, u32[]{:S(2)}) collective-permute-start(bf16[1416,128]{1,0:T(8,128)(2,1)S(1)} %get-tuple-element.53), channel_id=1, source_target_pairs={{0,10},{1,11},{2,8},{3,9},{4,14},{5,15},{6,12},{7,13},{8,2},{9,3},... | collective-permute-start | bytes 1087496 | tf_op jit(solution)/shard_map/ppermute | solution.py:209
  69.0 28.8 %collective-permute-start.7 = (bf16[1416,128]{1,0:T(8,128)(2,1)S(1)}, bf16[1416,128]{1,0:T(8,128)(2,1)S(1)}, u32[]{:S(2)}, u32[]{:S(2)}) collective-permute-start(bf16[1416,128]{1,0:T(8,128)(2,1)S(1)} %get-tuple-element.54), channel_id=1, source_target_pairs={{0,6},{1,7},{2,4},{3,5},{4,10},{5,11},{6,8},{7,9},{8,14},{9,15},{1... | collective-permute-start | bytes 1087496 | tf_op jit(solution)/shard_map/ppermute | solution.py:209
  77.5 21.6 %collective-permute-start.8 = (bf16[1416,128]{1,0:T(8,128)(2,1)S(1)}, bf16[1416,128]{1,0:T(8,128)(2,1)S(1)}, u32[]{:S(2)}, u32[]{:S(2)}) collective-permute-start(bf16[1416,128]{1,0:T(8,128)(2,1)S(1)} %get-tuple-element.55), channel_id=1, source_target_pairs={{0,12},{1,13},{2,14},{3,15},{4,0},{5,1},{6,2},{7,3},{8,4},{9,5},{1... | collective-permute-start | bytes 1087496 | tf_op jit(solution)/shard_map/ppermute | solution.py:209
  80.5 30.3 %collective-permute-start.9 = (bf16[1416,128]{1,0:T(8,128)(2,1)S(1)}, bf16[1416,128]{1,0:T(8,128)(2,1)S(1)}, u32[]{:S(2)}, u32[]{:S(2)}) collective-permute-start(bf16[1416,128]{1,0:T(8,128)(2,1)S(1)} %get-tuple-element.56), channel_id=1, source_target_pairs={{0,14},{1,15},{2,12},{3,13},{4,2},{5,3},{6,0},{7,1},{8,6},{9,7},{1... | collective-permute-start | bytes 1087496 | tf_op jit(solution)/shard_map/ppermute | solution.py:209
  93.8 63.0 %collective-permute-start.25 = (bf16[704,128]{1,0:T(8,128)(2,1)S(1)}, bf16[704,128]{1,0:T(8,128)(2,1)S(1)}, u32[]{:S(2)}, u32[]{:S(2)}) collective-permute-start(bf16[704,128]{1,0:T(8,128)(2,1)S(1)} %get-tuple-element.75), channel_id=1, source_target_pairs={{0,4},{1,5},{2,6},{3,7},{4,8},{5,9},{6,10},{7,11},{8,12},{9,13},{1... | collective-permute-start | bytes 540680 | tf_op jit(solution)/shard_map/ppermute | solution.py:209
  95.0 61.8 %collective-permute-start.26 = (bf16[704,128]{1,0:T(8,128)(2,1)S(1)}, bf16[704,128]{1,0:T(8,128)(2,1)S(1)}, u32[]{:S(2)}, u32[]{:S(2)}) collective-permute-start(bf16[704,128]{1,0:T(8,128)(2,1)S(1)} %get-tuple-element.76), channel_id=1, source_target_pairs={{0,9},{1,10},{2,11},{3,8},{4,13},{5,14},{6,15},{7,12},{8,1},{9,2},... | collective-permute-start | bytes 540680 | tf_op jit(solution)/shard_map/ppermute | solution.py:209
  97.8 59.1 %collective-permute-start.27 = (bf16[704,128]{1,0:T(8,128)(2,1)S(1)}, bf16[704,128]{1,0:T(8,128)(2,1)S(1)}, u32[]{:S(2)}, u32[]{:S(2)}) collective-permute-start(bf16[704,128]{1,0:T(8,128)(2,1)S(1)} %get-tuple-element.77), channel_id=1, source_target_pairs={{0,3},{1,0},{2,1},{3,2},{4,7},{5,4},{6,5},{7,6},{8,11},{9,8},{10,9... | collective-permute-start | bytes 540680 | tf_op jit(solution)/shard_map/ppermute | solution.py:209
  99.1 57.8 %collective-permute-start.28 = (bf16[704,128]{1,0:T(8,128)(2,1)S(1)}, bf16[704,128]{1,0:T(8,128)(2,1)S(1)}, u32[]{:S(2)}, u32[]{:S(2)}) collective-permute-start(bf16[704,128]{1,0:T(8,128)(2,1)S(1)} %get-tuple-element.78), channel_id=1, source_target_pairs={{0,11},{1,8},{2,9},{3,10},{4,15},{5,12},{6,13},{7,14},{8,3},{9,0},... | collective-permute-start | bytes 540680 | tf_op jit(solution)/shard_map/ppermute | solution.py:209
  110.8 46.0 %collective-permute-start.29 = (bf16[704,128]{1,0:T(8,128)(2,1)S(1)}, bf16[704,128]{1,0:T(8,128)(2,1)S(1)}, u32[]{:S(2)}, u32[]{:S(2)}) collective-permute-start(bf16[704,128]{1,0:T(8,128)(2,1)S(1)} %get-tuple-element.79), channel_id=1, source_target_pairs={{0,1},{1,2},{2,3},{3,0},{4,5},{5,6},{6,7},{7,4},{8,9},{9,10},{10,1... | collective-permute-start | bytes 540680 | tf_op jit(solution)/shard_map/ppermute | solution.py:209

commit v4 on v3

--- a/solution.py
+++ b/solution.py
@@ -162,13 +162,17 @@
     finish_kernel(me, parts, [(down, scale_down), (gate, scale_gate)], routed, made, sems)
 
 
-def finish_last_kernel(me, _, *rest):
-    parts, (up, scale_up, made, sems) = rest[:PEERS], rest[PEERS:]
+def finish_last_kernel(me, gathered, *rest):
+    parts, (up, scale_up, served, made, sems, sem) = rest[:PEERS], rest[PEERS:]
+    copy = pltpu.make_async_copy(gathered, served, sem)
+    copy.start()
     finish_kernel(me, parts, [(up, scale_up)], None, made, sems)
+    copy.wait()
 
 
 READY = jax.ShapeDtypeStruct((OWN, COLS, D_MODEL), jnp.bfloat16)
 SCALE = jax.ShapeDtypeStruct((OWN, COLS), jnp.float32)
+SERVED = jax.ShapeDtypeStruct((8 * OWN, D_MODEL), jnp.bfloat16)
 ROUTED = jax.ShapeDtypeStruct((OWN, D_MODEL), jnp.bfloat16)
 
 
@@ -187,19 +191,20 @@
     )(me, *parts)
 
 
-def finish_last(me, after, parts):
+def finish_last(me, gathered, parts):
     return pl.pallas_call(
         finish_last_kernel,
         in_specs=[SMEM, ANY] + [VMEM] * PEERS,
-        out_specs=[HBM, VMEM],
-        out_shape=[READY, SCALE],
+        out_specs=[HBM, VMEM, HBM],
+        out_shape=[READY, SCALE, SERVED],
         scratch_shapes=[
             pltpu.VMEM((OWN, COLS, D_MODEL), jnp.bfloat16),
             pltpu.SemaphoreType.DMA((OWN,)),
+            pltpu.SemaphoreType.DMA,
         ],
         compiler_params=pltpu.CompilerParams(vmem_limit_bytes=9 << 20),
         name="finish_last",
-    )(me, after, *parts)
+    )(me, gathered, *parts)
 
 
 def to_owners(parts):
@@ -218,8 +223,8 @@
     last = pack_last(me, train_up, first[0])
     got_last = to_owners(last)
     ready_down, scale_down, ready_gate, scale_gate, routed = finish_first(me, got_first)
-    serve_router = lax.all_gather(routed, "ep", axis=0, tiled=True)
-    ready_up, scale_up = finish_last(me, serve_router, got_last)
+    gathered = lax.all_gather(routed, "ep", axis=0, tiled=True)
+    ready_up, scale_up, serve_router = finish_last(me, gathered, got_last)
     return (
         jnp.swapaxes(ready_gate, 1, 2),
         jnp.swapaxes(ready_up, 1, 2),

time: 161 us -> 155 us (0.963)
  waiting for transfers between devices: 37 us -> 29.9 us
    ppermute x30, waiting for transfers between devices: 37 us -> 29.9 us  [to_owners(): received.append(lax.ppermute(parts[k + 1], 'fsdp', route))]
  transfers between devices with their start and end apart: 30 -> 30, of which waited for: 14 -> 11; matrix products, arithmetic and copies ran while one was open for 0% -> 0% of each run, Pallas kernels for 3% -> 3%
where the time goes in v4:
time: 155 us; the launch traced here: 154 us
  starting transfers between devices  62 us (40%)
  blocking collectives  42.6 us (27%)
  waiting for transfers between devices  29.9 us (19%)
  Pallas kernels  17 us (11%)
    ppermute x30, starting transfers between devices, to_owners(): received.append(lax.ppermute(parts[k + 1], 'fsdp', route))  62 us
    all_gather x1, blocking collectives, shards(): gathered = lax.all_gather(routed, 'ep', axis=0, tiled=True)  42.6 us
    ppermute x30, waiting for transfers between devices, to_owners(): received.append(lax.ppermute(parts[k + 1], 'fsdp', route))  29.9 us
    pallas_call x1, Pallas kernels, finish_first(): pl.pallas_call(finish_first_kernel, in_specs=[SMEM] + [VMEM] * PEERS, out...  4.94 us
    pallas_call x1, Pallas kernels, pack_first(): pl.pallas_call(pack_first_kernel, in_specs=[SMEM, HBM, HBM, VMEM], out_sp...  4.6 us
    pallas_call x1, Pallas kernels, pack_last(): pl.pallas_call(pack_last_kernel, in_specs=[SMEM, HBM, ANY], out_specs=[VM...  4.29 us
    pallas_call x1, Pallas kernels, finish_last(): pl.pallas_call(finish_last_kernel, in_specs=[SMEM, ANY] + [VMEM] * PEERS,...  3.19 us
  transfers between devices with their start and end apart: 30, of which 11 were waited for; matrix products, arithmetic and copies ran while one was open for 0% of the time, Pallas kernels for 3%

profile of v4, /device:TPU:23, one launch (start us, length us, event | category | flops | bytes accessed | tf_op | source)
XLA Modules:
  0.0 154.4 jit_solution(15667173900399409601)
XLA Ops:
  0.6 0.7 fusion.served
  1.3 4.6 %pack_first.1 = (bf16[1416,128]{1,0:T(8,128)(2,1)S(1)}, bf16[1416,128]{1,0:T(8,128)(2,1)S(1)}, bf16[1416,128]{1,0:T(8,128)(2,1)S(1)}, bf16[1416,128]{1,0:T(8,128...) custom-call(s32[1]{0:T(128)} %bitcast.me, ...), custom_call_target="tpu_custom_call" | custom-call | tf_op jit(solution)/shard_map/pack_first/pallas_call | solution.py:84
  5.9 1.4 copy-done
  7.3 4.3 %pack_last.1 = (bf16[704,128]{1,0:T(8,128)(2,1)S(1)}, bf16[704,128]{1,0:T(8,128)(2,1)S(1)}, bf16[704,128]{1,0:T(8,128)(2,1)S(1)}, bf16[704,128]{1,0:T(8,128)(2,1...) custom-call(s32[1]{0:T(128)} %bitcast.me, ...), custom_call_target="tpu_custom_call" | custom-call | tf_op jit(solution)/shard_map/pack_last/pallas_call | solution.py:113
  11.6 1.0 collective-permute-start.15
  12.6 1.4 collective-permute-start.16
  14.1 1.3 collective-permute-start.17
  15.4 1.1 collective-permute-start.18
  16.4 1.1 collective-permute-start.19
  17.6 0.5 collective-permute-done.15.rest_1_
  18.0 1.3 collective-permute-start.20
  19.3 1.5 collective-permute-done.16.rest_2_
  20.8 1.3 collective-permute-start.21
  22.1 1.9 %collective-permute-done.17.rest_3_ = bf16[704,128]{1,0:T(8,128)(2,1)S(1)} collective-permute-done((bf16[704,128]{1,0:T(8,128)(2,1)S(1)}, bf16[704,128]{1,0:T(8,128)(2,1)S(1)}, u32[]{:S(2)}, u32[]{:S(2)}) %collective-permute-start.17) | collective-permute-done | bytes 180256 | tf_op jit(solution)/shard_map/ppermute | solution.py:214
  24.0 1.4 collective-permute-start.22
  25.3 0.0 collective-permute-done.18.rest_4_
  25.3 0.8 collective-permute-start.23
  26.1 0.5 collective-permute-done.19.rest_5_
  26.6 2.0 %collective-permute-start.24 = (bf16[704,128]{1,0:T(8,128)(2,1)S(1)}, bf16[704,128]{1,0:T(8,128)(2,1)S(1)}, u32[]{:S(2)}, u32[]{:S(2)}) collective-permute-start(bf16[704,128]{1,0:T(8,128)(2,1)S(1)} %get-tuple-element.75), channel_id=1, source_target_pairs={{0,14},{1,15},{2,12},{3,13},{4,2},{5,3},{6,0},{7,1},{8,6},{9,7},{1... | collective-permute-start | bytes 540680 | tf_op jit(solution)/shard_map/ppermute | solution.py:214
  28.7 0.0 collective-permute-done.20.rest_6_
  28.7 1.9 %collective-permute-start = (bf16[1416,128]{1,0:T(8,128)(2,1)S(1)}, bf16[1416,128]{1,0:T(8,128)(2,1)S(1)}, u32[]{:S(2)}, u32[]{:S(2)}) collective-permute-start(bf16[1416,128]{1,0:T(8,128)(2,1)S(1)} %get-tuple-element.48), channel_id=1, source_target_pairs={{0,5},{1,6},{2,7},{3,4},{4,9},{5,10},{6,11},{7,8},{8,13},{9,14},{1... | collective-permute-start | bytes 1087496 | tf_op jit(solution)/shard_map/ppermute | solution.py:214
  30.6 0.9 collective-permute-done.21.rest_7_
  31.5 0.3 collective-permute-start.1
  31.8 2.0 %collective-permute-done.22.rest_8_ = bf16[704,128]{1,0:T(8,128)(2,1)S(1)} collective-permute-done((bf16[704,128]{1,0:T(8,128)(2,1)S(1)}, bf16[704,128]{1,0:T(8,128)(2,1)S(1)}, u32[]{:S(2)}, u32[]{:S(2)}) %collective-permute-start.22) | collective-permute-done | bytes 180256 | tf_op jit(solution)/shard_map/ppermute | solution.py:214
  33.7 4.0 %collective-permute-start.2 = (bf16[1416,128]{1,0:T(8,128)(2,1)S(1)}, bf16[1416,128]{1,0:T(8,128)(2,1)S(1)}, u32[]{:S(2)}, u32[]{:S(2)}) collective-permute-start(bf16[1416,128]{1,0:T(8,128)(2,1)S(1)} %get-tuple-element.50), channel_id=1, source_target_pairs={{0,13},{1,14},{2,15},{3,12},{4,1},{5,2},{6,3},{7,0},{8,5},{9,6},{1... | collective-permute-start | bytes 1087496 | tf_op jit(solution)/shard_map/ppermute | solution.py:214
  37.8 0.0 collective-permute-done.23.rest_9_
  37.8 1.4 collective-permute-start.3
  39.2 0.0 collective-permute-done.24.rest_10_
  39.2 1.6 %collective-permute-start.4 = (bf16[1416,128]{1,0:T(8,128)(2,1)S(1)}, bf16[1416,128]{1,0:T(8,128)(2,1)S(1)}, u32[]{:S(2)}, u32[]{:S(2)}) collective-permute-start(bf16[1416,128]{1,0:T(8,128)(2,1)S(1)} %get-tuple-element.52), channel_id=1, source_target_pairs={{0,2},{1,3},{2,0},{3,1},{4,6},{5,7},{6,4},{7,5},{8,10},{9,11},{10,... | collective-permute-start | bytes 1087496 | tf_op jit(solution)/shard_map/ppermute | solution.py:214
  40.8 0.7 collective-permute-done.rest_1_
  41.5 8.6 %collective-permute-start.5 = (bf16[1416,128]{1,0:T(8,128)(2,1)S(1)}, bf16[1416,128]{1,0:T(8,128)(2,1)S(1)}, u32[]{:S(2)}, u32[]{:S(2)}) collective-permute-start(bf16[1416,128]{1,0:T(8,128)(2,1)S(1)} %get-tuple-element.53), channel_id=1, source_target_pairs={{0,8},{1,9},{2,10},{3,11},{4,12},{5,13},{6,14},{7,15},{8,0},{9,1},... | collective-permute-start | bytes 1087496 | tf_op jit(solution)/shard_map/ppermute | solution.py:214
  50.1 0.0 collective-permute-done.1.rest_2_
  50.1 2.7 %collective-permute-start.6 = (bf16[1416,128]{1,0:T(8,128)(2,1)S(1)}, bf16[1416,128]{1,0:T(8,128)(2,1)S(1)}, u32[]{:S(2)}, u32[]{:S(2)}) collective-permute-start(bf16[1416,128]{1,0:T(8,128)(2,1)S(1)} %get-tuple-element.54), channel_id=1, source_target_pairs={{0,10},{1,11},{2,8},{3,9},{4,14},{5,15},{6,12},{7,13},{8,2},{9,3},... | collective-permute-start | bytes 1087496 | tf_op jit(solution)/shard_map/ppermute | solution.py:214
  52.8 0.0 collective-permute-done.2.rest_3_
  52.8 0.0 collective-permute-start.7
  52.8 0.0 collective-permute-done.3.rest_4_
  52.8 1.5 collective-permute-start.8
  54.2 1.2 collective-permute-done.4.rest_5_
  55.5 1.3 collective-permute-start.9
  56.7 0.7 collective-permute-done.5.rest_6_
  57.5 13.3 %collective-permute-start.10 = (bf16[1416,128]{1,0:T(8,128)(2,1)S(1)}, bf16[1416,128]{1,0:T(8,128)(2,1)S(1)}, u32[]{:S(2)}, u32[]{:S(2)}) collective-permute-start(bf16[1416,128]{1,0:T(8,128)(2,1)S(1)} %get-tuple-element.58), channel_id=1, source_target_pairs={{0,4},{1,5},{2,6},{3,7},{4,8},{5,9},{6,10},{7,11},{8,12},{9,13},{1... | collective-permute-start | bytes 1087496 | tf_op jit(solution)/shard_map/ppermute | solution.py:214
  70.8 0.0 collective-permute-done.6.rest_7_
  70.8 0.5 collective-permute-start.11
  71.3 0.0 collective-permute-done.7.rest_8_
  71.3 3.2 %collective-permute-start.12 = (bf16[1416,128]{1,0:T(8,128)(2,1)S(1)}, bf16[1416,128]{1,0:T(8,128)(2,1)S(1)}, u32[]{:S(2)}, u32[]{:S(2)}) collective-permute-start(bf16[1416,128]{1,0:T(8,128)(2,1)S(1)} %get-tuple-element.60), channel_id=1, source_target_pairs={{0,3},{1,0},{2,1},{3,2},{4,7},{5,4},{6,5},{7,6},{8,11},{9,8},{10,9... | collective-permute-start | bytes 1087496 | tf_op jit(solution)/shard_map/ppermute | solution.py:214
  74.4 3.8 %collective-permute-done.8.rest_9_ = bf16[1416,128]{1,0:T(8,128)(2,1)S(1)} collective-permute-done((bf16[1416,128]{1,0:T(8,128)(2,1)S(1)}, bf16[1416,128]{1,0:T(8,128)(2,1)S(1)}, u32[]{:S(2)}, u32[]{:S(2)}) %collective-permute-start.8) | collective-permute-done | bytes 362528 | tf_op jit(solution)/shard_map/ppermute | solution.py:214
  78.2 0.0 collective-permute-start.13
  78.2 0.0 collective-permute-done.9.rest_10_
  78.3 0.0 collective-permute-start.14
  78.3 16.1 %collective-permute-done.10.rest_11_ = bf16[1416,128]{1,0:T(8,128)(2,1)S(1)} collective-permute-done((bf16[1416,128]{1,0:T(8,128)(2,1)S(1)}, bf16[1416,128]{1,0:T(8,128)(2,1)S(1)}, u32[]{:S(2)}, u32[]{:S(2)}) %collective-permute-start.10) | collective-permute-done | bytes 362528 | tf_op jit(solution)/shard_map/ppermute | solution.py:214
  94.4 0.0 collective-permute-start.25
  94.4 0.0 collective-permute-done.11.rest_12_
  94.4 0.0 collective-permute-start.26
  94.4 0.0 collective-permute-done.12.rest_13_
  94.4 7.7 %collective-permute-start.27 = (bf16[704,128]{1,0:T(8,128)(2,1)S(1)}, bf16[704,128]{1,0:T(8,128)(2,1)S(1)}, u32[]{:S(2)}, u32[]{:S(2)}) collective-permute-start(bf16[704,128]{1,0:T(8,128)(2,1)S(1)} %get-tuple-element.78), channel_id=1, source_target_pairs={{0,3},{1,0},{2,1},{3,2},{4,7},{5,4},{6,5},{7,6},{8,11},{9,8},{10,9... | collective-permute-start | bytes 540680 | tf_op jit(solution)/shard_map/ppermute | solution.py:214
  102.1 0.0 collective-permute-done.13.rest_14_
  102.1 0.0 collective-permute-start.28
  102.1 0.0 collective-permute-done.14.rest_15_
  102.2 1.4 collective-permute-start.29
  103.5 4.9 %finish_first.1 = (bf16[8,88,2048]{2,1,0:T(8,128)(2,1)}, f32[8,88]{1,0:T(8,128)}, bf16[8,88,2048]{2,1,0:T(8,128)(2,1)}, f32[8,88]{1,0:T(8,128)}, bf16[8,2048]{1,0:T(8,128)(2,1)S(1)}) custom-call(s32[1]{0:T(128)} %bitcast.me, bf16[1416,128]{1,0:T(8,128)(2,1)S(1)} %get-tuple-element.47.rest_0_._, bf16[1416,128]{1,0:T(8,128)(2,1)S(1)} %collective-permute-done.rest_1_, ...), custom_call_target="tpu_custom_call" | custom-call | tf_op jit(solution)/shard_map/finish_first/pallas_call | solution.py:180
  108.5 42.6 %all_gather.3.gathered = bf16[64,2048]{1,0:T(8,128)(2,1)S(1)} all-gather(bf16[8,2048]{1,0:T(8,128)(2,1)S(1)} %get-tuple-element.64), channel_id=1, replica_groups=mesh['ep'=8,'fsdp'=16] {'ep'}, dimensions={0}, use_global_device_ids=true | all-gather | bytes 294912 | tf_op jit(solution)/shard_map/all_gather | solution.py:226
  151.0 0.0 collective-permute-done.25.rest_11_
  151.0 0.0 collective-permute-done.26.rest_12_
  151.1 3.2 %finish_last.1 = (bf16[8,88,2048]{2,1,0:T(8,128)(2,1)}, f32[8,88]{1,0:T(8,128)}, bf16[64,2048]{1,0:T(8,128)(2,1)}) custom-call(s32[1]{0:T(128)} %bitcast.me, bf16[64,2048]{1,0:T(8,128)(2,1)S(1)} %all_gather.3.gathered, bf16[704,128]{1,0:T(8,128)(2,1)S(1)} %get-tuple-element.65.rest_0_, bf16[704,128]{1,0:T(8,128)(2,1)S(1)} %collective-permute-done.15.rest_1_, ...), custom_call_target="tpu_custom_call" | custom-call | tf_op jit(solution)/shard_map/finish_last/pallas_call | solution.py:195
  (4 shorter events, 0.0 us)
Async XLA Ops:
  1.3 6.0 %copy-start = (f32[8,128,1408]{2,1,0:T(8,128)S(1)}, f32[8,128,1408]{2,1,0:T(8,128)}, u32[]{:S(2)}) copy-start(f32[8,128,1408]{2,1,0:T(8,128)} %up.1) | copy-start | bytes 17301508
  11.6 6.4 %collective-permute-start.15 = (bf16[704,128]{1,0:T(8,128)(2,1)S(1)}, bf16[704,128]{1,0:T(8,128)(2,1)S(1)}, u32[]{:S(2)}, u32[]{:S(2)}) collective-permute-start(bf16[704,128]{1,0:T(8,128)(2,1)S(1)} %get-tuple-element.66), channel_id=1, source_target_pairs={{0,5},{1,6},{2,7},{3,4},{4,9},{5,10},{6,11},{7,8},{8,13},{9,14},{1... | collective-permute-start | bytes 540680 | tf_op jit(solution)/shard_map/ppermute | solution.py:214
  12.6 8.2 %collective-permute-start.16 = (bf16[704,128]{1,0:T(8,128)(2,1)S(1)}, bf16[704,128]{1,0:T(8,128)(2,1)S(1)}, u32[]{:S(2)}, u32[]{:S(2)}) collective-permute-start(bf16[704,128]{1,0:T(8,128)(2,1)S(1)} %get-tuple-element.67), channel_id=1, source_target_pairs={{0,15},{1,12},{2,13},{3,14},{4,3},{5,0},{6,1},{7,2},{8,7},{9,4},{1... | collective-permute-start | bytes 540680 | tf_op jit(solution)/shard_map/ppermute | solution.py:214
  14.1 9.9 %collective-permute-start.17 = (bf16[704,128]{1,0:T(8,128)(2,1)S(1)}, bf16[704,128]{1,0:T(8,128)(2,1)S(1)}, u32[]{:S(2)}, u32[]{:S(2)}) collective-permute-start(bf16[704,128]{1,0:T(8,128)(2,1)S(1)} %get-tuple-element.68), channel_id=1, source_target_pairs={{0,13},{1,14},{2,15},{3,12},{4,1},{5,2},{6,3},{7,0},{8,5},{9,6},{1... | collective-permute-start | bytes 540680 | tf_op jit(solution)/shard_map/ppermute | solution.py:214
  15.4 10.0 %collective-permute-start.18 = (bf16[704,128]{1,0:T(8,128)(2,1)S(1)}, bf16[704,128]{1,0:T(8,128)(2,1)S(1)}, u32[]{:S(2)}, u32[]{:S(2)}) collective-permute-start(bf16[704,128]{1,0:T(8,128)(2,1)S(1)} %get-tuple-element.69), channel_id=1, source_target_pairs={{0,7},{1,4},{2,5},{3,6},{4,11},{5,8},{6,9},{7,10},{8,15},{9,12},{1... | collective-permute-start | bytes 540680 | tf_op jit(solution)/shard_map/ppermute | solution.py:214
  16.4 10.2 %collective-permute-start.19 = (bf16[704,128]{1,0:T(8,128)(2,1)S(1)}, bf16[704,128]{1,0:T(8,128)(2,1)S(1)}, u32[]{:S(2)}, u32[]{:S(2)}) collective-permute-start(bf16[704,128]{1,0:T(8,128)(2,1)S(1)} %get-tuple-element.70), channel_id=1, source_target_pairs={{0,2},{1,3},{2,0},{3,1},{4,6},{5,7},{6,4},{7,5},{8,10},{9,11},{10,... | collective-permute-start | bytes 540680 | tf_op jit(solution)/shard_map/ppermute | solution.py:214
  18.0 10.6 %collective-permute-start.20 = (bf16[704,128]{1,0:T(8,128)(2,1)S(1)}, bf16[704,128]{1,0:T(8,128)(2,1)S(1)}, u32[]{:S(2)}, u32[]{:S(2)}) collective-permute-start(bf16[704,128]{1,0:T(8,128)(2,1)S(1)} %get-tuple-element.71), channel_id=1, source_target_pairs={{0,8},{1,9},{2,10},{3,11},{4,12},{5,13},{6,14},{7,15},{8,0},{9,1},... | collective-permute-start | bytes 540680 | tf_op jit(solution)/shard_map/ppermute | solution.py:214
  20.8 10.7 %collective-permute-start.21 = (bf16[704,128]{1,0:T(8,128)(2,1)S(1)}, bf16[704,128]{1,0:T(8,128)(2,1)S(1)}, u32[]{:S(2)}, u32[]{:S(2)}) collective-permute-start(bf16[704,128]{1,0:T(8,128)(2,1)S(1)} %get-tuple-element.72), channel_id=1, source_target_pairs={{0,10},{1,11},{2,8},{3,9},{4,14},{5,15},{6,12},{7,13},{8,2},{9,3},... | collective-permute-start | bytes 540680 | tf_op jit(solution)/shard_map/ppermute | solution.py:214
  24.0 9.7 %collective-permute-start.22 = (bf16[704,128]{1,0:T(8,128)(2,1)S(1)}, bf16[704,128]{1,0:T(8,128)(2,1)S(1)}, u32[]{:S(2)}, u32[]{:S(2)}) collective-permute-start(bf16[704,128]{1,0:T(8,128)(2,1)S(1)} %get-tuple-element.73), channel_id=1, source_target_pairs={{0,6},{1,7},{2,4},{3,5},{4,10},{5,11},{6,8},{7,9},{8,14},{9,15},{1... | collective-permute-start | bytes 540680 | tf_op jit(solution)/shard_map/ppermute | solution.py:214
  25.3 12.4 %collective-permute-start.23 = (bf16[704,128]{1,0:T(8,128)(2,1)S(1)}, bf16[704,128]{1,0:T(8,128)(2,1)S(1)}, u32[]{:S(2)}, u32[]{:S(2)}) collective-permute-start(bf16[704,128]{1,0:T(8,128)(2,1)S(1)} %get-tuple-element.74), channel_id=1, source_target_pairs={{0,12},{1,13},{2,14},{3,15},{4,0},{5,1},{6,2},{7,3},{8,4},{9,5},{1... | collective-permute-start | bytes 540680 | tf_op jit(solution)/shard_map/ppermute | solution.py:214
  26.6 12.5 %collective-permute-start.24 = (bf16[704,128]{1,0:T(8,128)(2,1)S(1)}, bf16[704,128]{1,0:T(8,128)(2,1)S(1)}, u32[]{:S(2)}, u32[]{:S(2)}) collective-permute-start(bf16[704,128]{1,0:T(8,128)(2,1)S(1)} %get-tuple-element.75), channel_id=1, source_target_pairs={{0,14},{1,15},{2,12},{3,13},{4,2},{5,3},{6,0},{7,1},{8,6},{9,7},{1... | collective-permute-start | bytes 540680 | tf_op jit(solution)/shard_map/ppermute | solution.py:214
  28.7 12.8 %collective-permute-start = (bf16[1416,128]{1,0:T(8,128)(2,1)S(1)}, bf16[1416,128]{1,0:T(8,128)(2,1)S(1)}, u32[]{:S(2)}, u32[]{:S(2)}) collective-permute-start(bf16[1416,128]{1,0:T(8,128)(2,1)S(1)} %get-tuple-element.48), channel_id=1, source_target_pairs={{0,5},{1,6},{2,7},{3,4},{4,9},{5,10},{6,11},{7,8},{8,13},{9,14},{1... | collective-permute-start | bytes 1087496 | tf_op jit(solution)/shard_map/ppermute | solution.py:214
  31.5 18.6 %collective-permute-start.1 = (bf16[1416,128]{1,0:T(8,128)(2,1)S(1)}, bf16[1416,128]{1,0:T(8,128)(2,1)S(1)}, u32[]{:S(2)}, u32[]{:S(2)}) collective-permute-start(bf16[1416,128]{1,0:T(8,128)(2,1)S(1)} %get-tuple-element.49), channel_id=1, source_target_pairs={{0,15},{1,12},{2,13},{3,14},{4,3},{5,0},{6,1},{7,2},{8,7},{9,4},{1... | collective-permute-start | bytes 1087496 | tf_op jit(solution)/shard_map/ppermute | solution.py:214
  33.7 19.1 %collective-permute-start.2 = (bf16[1416,128]{1,0:T(8,128)(2,1)S(1)}, bf16[1416,128]{1,0:T(8,128)(2,1)S(1)}, u32[]{:S(2)}, u32[]{:S(2)}) collective-permute-start(bf16[1416,128]{1,0:T(8,128)(2,1)S(1)} %get-tuple-element.50), channel_id=1, source_target_pairs={{0,13},{1,14},{2,15},{3,12},{4,1},{5,2},{6,3},{7,0},{8,5},{9,6},{1... | collective-permute-start | bytes 1087496 | tf_op jit(solution)/shard_map/ppermute | solution.py:214
  37.8 15.0 %collective-permute-start.3 = (bf16[1416,128]{1,0:T(8,128)(2,1)S(1)}, bf16[1416,128]{1,0:T(8,128)(2,1)S(1)}, u32[]{:S(2)}, u32[]{:S(2)}) collective-permute-start(bf16[1416,128]{1,0:T(8,128)(2,1)S(1)} %get-tuple-element.51), channel_id=1, source_target_pairs={{0,7},{1,4},{2,5},{3,6},{4,11},{5,8},{6,9},{7,10},{8,15},{9,12},{1... | collective-permute-start | bytes 1087496 | tf_op jit(solution)/shard_map/ppermute | solution.py:214
  39.2 16.3 %collective-permute-start.4 = (bf16[1416,128]{1,0:T(8,128)(2,1)S(1)}, bf16[1416,128]{1,0:T(8,128)(2,1)S(1)}, u32[]{:S(2)}, u32[]{:S(2)}) collective-permute-start(bf16[1416,128]{1,0:T(8,128)(2,1)S(1)} %get-tuple-element.52), channel_id=1, source_target_pairs={{0,2},{1,3},{2,0},{3,1},{4,6},{5,7},{6,4},{7,5},{8,10},{9,11},{10,... | collective-permute-start | bytes 1087496 | tf_op jit(solution)/shard_map/ppermute | solution.py:214
  41.5 16.0 %collective-permute-start.5 = (bf16[1416,128]{1,0:T(8,128)(2,1)S(1)}, bf16[1416,128]{1,0:T(8,128)(2,1)S(1)}, u32[]{:S(2)}, u32[]{:S(2)}) collective-permute-start(bf16[1416,128]{1,0:T(8,128)(2,1)S(1)} %get-tuple-element.53), channel_id=1, source_target_pairs={{0,8},{1,9},{2,10},{3,11},{4,12},{5,13},{6,14},{7,15},{8,0},{9,1},... | collective-permute-start | bytes 1087496 | tf_op jit(solution)/shard_map/ppermute | solution.py:214
  50.1 20.7 %collective-permute-start.6 = (bf16[1416,128]{1,0:T(8,128)(2,1)S(1)}, bf16[1416,128]{1,0:T(8,128)(2,1)S(1)}, u32[]{:S(2)}, u32[]{:S(2)}) collective-permute-start(bf16[1416,128]{1,0:T(8,128)(2,1)S(1)} %get-tuple-element.54), channel_id=1, source_target_pairs={{0,10},{1,11},{2,8},{3,9},{4,14},{5,15},{6,12},{7,13},{8,2},{9,3},... | collective-permute-start | bytes 1087496 | tf_op jit(solution)/shard_map/ppermute | solution.py:214
  52.8 18.5 %collective-permute-start.7 = (bf16[1416,128]{1,0:T(8,128)(2,1)S(1)}, bf16[1416,128]{1,0:T(8,128)(2,1)S(1)}, u32[]{:S(2)}, u32[]{:S(2)}) collective-permute-start(bf16[1416,128]{1,0:T(8,128)(2,1)S(1)} %get-tuple-element.55), channel_id=1, source_target_pairs={{0,6},{1,7},{2,4},{3,5},{4,10},{5,11},{6,8},{7,9},{8,14},{9,15},{1... | collective-permute-start | bytes 1087496 | tf_op jit(solution)/shard_map/ppermute | solution.py:214
  52.8 25.4 %collective-permute-start.8 = (bf16[1416,128]{1,0:T(8,128)(2,1)S(1)}, bf16[1416,128]{1,0:T(8,128)(2,1)S(1)}, u32[]{:S(2)}, u32[]{:S(2)}) collective-permute-start(bf16[1416,128]{1,0:T(8,128)(2,1)S(1)} %get-tuple-element.56), channel_id=1, source_target_pairs={{0,12},{1,13},{2,14},{3,15},{4,0},{5,1},{6,2},{7,3},{8,4},{9,5},{1... | collective-permute-start | bytes 1087496 | tf_op jit(solution)/shard_map/ppermute | solution.py:214
  55.5 22.8 %collective-permute-start.9 = (bf16[1416,128]{1,0:T(8,128)(2,1)S(1)}, bf16[1416,128]{1,0:T(8,128)(2,1)S(1)}, u32[]{:S(2)}, u32[]{:S(2)}) collective-permute-start(bf16[1416,128]{1,0:T(8,128)(2,1)S(1)} %get-tuple-element.57), channel_id=1, source_target_pairs={{0,14},{1,15},{2,12},{3,13},{4,2},{5,3},{6,0},{7,1},{8,6},{9,7},{1... | collective-permute-start | bytes 1087496 | tf_op jit(solution)/shard_map/ppermute | solution.py:214
  57.5 36.9 %collective-permute-start.10 = (bf16[1416,128]{1,0:T(8,128)(2,1)S(1)}, bf16[1416,128]{1,0:T(8,128)(2,1)S(1)}, u32[]{:S(2)}, u32[]{:S(2)}) collective-permute-start(bf16[1416,128]{1,0:T(8,128)(2,1)S(1)} %get-tuple-element.58), channel_id=1, source_target_pairs={{0,4},{1,5},{2,6},{3,7},{4,8},{5,9},{6,10},{7,11},{8,12},{9,13},{1... | collective-permute-start | bytes 1087496 | tf_op jit(solution)/shard_map/ppermute | solution.py:214
  70.8 23.6 %collective-permute-start.11 = (bf16[1416,128]{1,0:T(8,128)(2,1)S(1)}, bf16[1416,128]{1,0:T(8,128)(2,1)S(1)}, u32[]{:S(2)}, u32[]{:S(2)}) collective-permute-start(bf16[1416,128]{1,0:T(8,128)(2,1)S(1)} %get-tuple-element.59), channel_id=1, source_target_pairs={{0,9},{1,10},{2,11},{3,8},{4,13},{5,14},{6,15},{7,12},{8,1},{9,2},... | collective-permute-start | bytes 1087496 | tf_op jit(solution)/shard_map/ppermute | solution.py:214
  71.3 23.2 %collective-permute-start.12 = (bf16[1416,128]{1,0:T(8,128)(2,1)S(1)}, bf16[1416,128]{1,0:T(8,128)(2,1)S(1)}, u32[]{:S(2)}, u32[]{:S(2)}) collective-permute-start(bf16[1416,128]{1,0:T(8,128)(2,1)S(1)} %get-tuple-element.60), channel_id=1, source_target_pairs={{0,3},{1,0},{2,1},{3,2},{4,7},{5,4},{6,5},{7,6},{8,11},{9,8},{10,9... | collective-permute-start | bytes 1087496 | tf_op jit(solution)/shard_map/ppermute | solution.py:214
  78.2 23.9 %collective-permute-start.13 = (bf16[1416,128]{1,0:T(8,128)(2,1)S(1)}, bf16[1416,128]{1,0:T(8,128)(2,1)S(1)}, u32[]{:S(2)}, u32[]{:S(2)}) collective-permute-start(bf16[1416,128]{1,0:T(8,128)(2,1)S(1)} %get-tuple-element.61), channel_id=1, source_target_pairs={{0,11},{1,8},{2,9},{3,10},{4,15},{5,12},{6,13},{7,14},{8,3},{9,0},... | collective-permute-start | bytes 1087496 | tf_op jit(solution)/shard_map/ppermute | solution.py:214
  78.3 23.9 %collective-permute-start.14 = (bf16[1416,128]{1,0:T(8,128)(2,1)S(1)}, bf16[1416,128]{1,0:T(8,128)(2,1)S(1)}, u32[]{:S(2)}, u32[]{:S(2)}) collective-permute-start(bf16[1416,128]{1,0:T(8,128)(2,1)S(1)} %get-tuple-element.62), channel_id=1, source_target_pairs={{0,1},{1,2},{2,3},{3,0},{4,5},{5,6},{6,7},{7,4},{8,9},{9,10},{10,1... | collective-permute-start | bytes 1087496 | tf_op jit(solution)/shard_map/ppermute | solution.py:214
  94.4 56.6 %collective-permute-start.25 = (bf16[704,128]{1,0:T(8,128)(2,1)S(1)}, bf16[704,128]{1,0:T(8,128)(2,1)S(1)}, u32[]{:S(2)}, u32[]{:S(2)}) collective-permute-start(bf16[704,128]{1,0:T(8,128)(2,1)S(1)} %get-tuple-element.76), channel_id=1, source_target_pairs={{0,4},{1,5},{2,6},{3,7},{4,8},{5,9},{6,10},{7,11},{8,12},{9,13},{1... | collective-permute-start | bytes 540680 | tf_op jit(solution)/shard_map/ppermute | solution.py:214
  94.4 56.6 %collective-permute-start.26 = (bf16[704,128]{1,0:T(8,128)(2,1)S(1)}, bf16[704,128]{1,0:T(8,128)(2,1)S(1)}, u32[]{:S(2)}, u32[]{:S(2)}) collective-permute-start(bf16[704,128]{1,0:T(8,128)(2,1)S(1)} %get-tuple-element.77), channel_id=1, source_target_pairs={{0,9},{1,10},{2,11},{3,8},{4,13},{5,14},{6,15},{7,12},{8,1},{9,2},... | collective-permute-start | bytes 540680 | tf_op jit(solution)/shard_map/ppermute | solution.py:214
  94.4 56.6 %collective-permute-start.27 = (bf16[704,128]{1,0:T(8,128)(2,1)S(1)}, bf16[704,128]{1,0:T(8,128)(2,1)S(1)}, u32[]{:S(2)}, u32[]{:S(2)}) collective-permute-start(bf16[704,128]{1,0:T(8,128)(2,1)S(1)} %get-tuple-element.78), channel_id=1, source_target_pairs={{0,3},{1,0},{2,1},{3,2},{4,7},{5,4},{6,5},{7,6},{8,11},{9,8},{10,9... | collective-permute-start | bytes 540680 | tf_op jit(solution)/shard_map/ppermute | solution.py:214
  102.1 48.9 %collective-permute-start.28 = (bf16[704,128]{1,0:T(8,128)(2,1)S(1)}, bf16[704,128]{1,0:T(8,128)(2,1)S(1)}, u32[]{:S(2)}, u32[]{:S(2)}) collective-permute-start(bf16[704,128]{1,0:T(8,128)(2,1)S(1)} %get-tuple-element.79), channel_id=1, source_target_pairs={{0,11},{1,8},{2,9},{3,10},{4,15},{5,12},{6,13},{7,14},{8,3},{9,0},... | collective-permute-start | bytes 540680 | tf_op jit(solution)/shard_map/ppermute | solution.py:214
  102.2 48.9 %collective-permute-start.29 = (bf16[704,128]{1,0:T(8,128)(2,1)S(1)}, bf16[704,128]{1,0:T(8,128)(2,1)S(1)}, u32[]{:S(2)}, u32[]{:S(2)}) collective-permute-start(bf16[704,128]{1,0:T(8,128)(2,1)S(1)} %get-tuple-element.80), channel_id=1, source_target_pairs={{0,1},{1,2},{2,3},{3,0},{4,5},{5,6},{6,7},{7,4},{8,9},{9,10},{10,1... | collective-permute-start | bytes 540680 | tf_op jit(solution)/shard_map/ppermute | solution.py:214
